TPU v7x, 32 devices: a whole 2x2x4 slice. The times are simulated.
32 devices in a mesh: groups: 2 (over y), fibre: 4 (over z), seg: 2 (over x), rec: 2 (over core).
Axes of the slice: x: 2, y: 2, z: 4, core: 2. Of those that a mesh axis runs over, the one named last changes fastest.
Arguments:
- records: bfloat16 [2, 2048, 1024], P('rec', 'fibre', ('groups', 'seg')), parts along dimension 2, may hold values from -6 to 6
- pairs: int32 [16, 2], replicated, may hold values from 0 to 15
- observed: float32 [32, 32, 256], P(('groups', 'fibre', 'seg')), parts along dimension 0, may hold values from -6 to 6
- lag_mask: int32 [32, 256], P(('groups', 'fibre', 'seg')), parts along dimension 0, may hold values 0 or 1
Outputs:
- adjoint_sources: bfloat16 [2, 2048, 1024], P('rec', 'fibre', ('groups', 'seg')), parts along dimension 2
There are 2 independent parts, one for each index of `groups`. A program takes and returns all parts, laid end to end along the dimension named above; an argument that names none is the same for every part. Nothing has to cross between parts.
All inputs are finite; a program needn't handle non-finite values. No bound on the sum of `lag_mask` on one device may be relied on, other than what follows from the above.
Results may differ from a plain program's by a relative error of at most 0.015.
Values may be sent and summed in bfloat16 or wider, within the bound.
A program may use at most 64 MiB of HBM per device.

v0:
```python
import functools

import jax
import jax.numpy as jnp
import numpy as np
from jax import lax
from jax.experimental import pallas as pl
from jax.experimental.pallas import tpu as pltpu
from jax.sharding import PartitionSpec as P

S = 2048
F = 1024
LAGS = 256
BLOCK = 32
CH_DEV = 64
VMEM_GRANT = 60899328


def forward_table():
    freq_index = jnp.arange(F, dtype=jnp.int32)
    time_index = jnp.arange(S, dtype=jnp.int32)
    phase = freq_index[:, None] * time_index[None, :] % S
    angles = phase.astype(jnp.float32) * (2.0 * jnp.pi / S)
    scale = 1.0 / jnp.sqrt(jnp.float32(S))
    return jnp.stack(
        [
            (jnp.cos(angles) * scale).astype(jnp.bfloat16),
            (-jnp.sin(angles) * scale).astype(jnp.bfloat16),
        ],
        axis=1,
    )


def lag_table():
    freq_index = jnp.arange(F, dtype=jnp.int32)
    shifts = (jnp.arange(LAGS, dtype=jnp.int32) - LAGS // 2) % S
    phase = freq_index[:, None] * shifts[None, :] % S
    angles = phase.astype(jnp.float32) * (2.0 * jnp.pi / S)
    scale = 1.0 / jnp.sqrt(jnp.float32(F))
    return jnp.stack(
        [
            (jnp.cos(angles) * scale).astype(jnp.bfloat16),
            (-jnp.sin(angles) * scale).astype(jnp.bfloat16),
        ],
        axis=1,
    )


def synthesize(incoming, table):
    count = incoming.shape[-1]
    flat = incoming.reshape(2 * F, count)
    result = jnp.einsum(
        "qn,qt->tn", flat, table.reshape(2 * F, S), preferred_element_type=jnp.float32
    )
    return result.astype(jnp.bfloat16)


def on_device(records, pairs, observed, lag_mask):
    fibre_count = lax.axis_size("fibre")
    seg_count = lax.axis_size("seg")
    spread_count = fibre_count * seg_count
    freq_dev = F // spread_count
    blocks_dev = CH_DEV // BLOCK
    block_count = CH_DEV * spread_count // BLOCK
    pair_total = pairs.shape[0]
    pairs_dev = pair_total // spread_count
    table = forward_table()
    lags = lag_table()
    spans = records.reshape(1, S // fibre_count, fibre_count, CH_DEV)
    incoming = lax.all_to_all(spans, "fibre", split_axis=2, concat_axis=1, tiled=True)
    count = incoming.shape[3]
    signal = incoming.reshape(S, count)
    result = jnp.einsum(
        "qs,sn->qn", table.reshape(2 * F, S), signal, preferred_element_type=jnp.float32
    )
    spectra = result.reshape(F, 2, count).astype(jnp.bfloat16)
    widened = lax.all_to_all(spectra, ("fibre", "seg"), split_axis=0, concat_axis=2, tiled=True)
    seg_blocks = fibre_count * blocks_dev
    slot_ids = (
        pairs % seg_blocks // blocks_dev * seg_count + pairs // seg_blocks
    ) * blocks_dev + pairs % blocks_dev
    blocks_grid = widened.reshape(freq_dev, 2, block_count, BLOCK)
    first_side = jnp.take(blocks_grid, slot_ids[:, 0], axis=2).astype(jnp.float32)
    second_side = jnp.take(blocks_grid, slot_ids[:, 1], axis=2).astype(jnp.float32)
    first_re, first_im = (first_side[:, 0], first_side[:, 1])
    second_re, second_im = (second_side[:, 0], second_side[:, 1])
    cross_re = first_re * second_re + first_im * second_im
    cross_im = first_im * second_re - first_re * second_im
    cross_spec = jnp.stack([cross_re, cross_im], axis=1).astype(jnp.bfloat16)
    cross_spec = cross_spec.reshape(freq_dev, 2, spread_count, pairs_dev * BLOCK)
    owned_spec = lax.all_to_all(
        cross_spec, ("fibre", "seg"), split_axis=2, concat_axis=0, tiled=True
    )
    owned_spec = owned_spec.reshape(F, 2, pairs_dev * BLOCK)
    partial_corr = jnp.einsum("wpx,wpl->xl", owned_spec, lags, preferred_element_type=jnp.float32)
    synthetic = (
        lax.psum(partial_corr.astype(jnp.bfloat16), "rec")
        .astype(jnp.float32)
        .reshape(pairs_dev, BLOCK, LAGS)
    )
    weights = lag_mask[:, None, :].astype(jnp.float32) * jnp.tanh(synthetic - observed)
    weights_low = weights.astype(jnp.bfloat16).reshape(pairs_dev * BLOCK, LAGS)
    adjoint_spec = jnp.einsum("xl,wpl->wpx", weights_low, lags, preferred_element_type=jnp.float32)
    adjoint_spec = adjoint_spec.astype(jnp.bfloat16).reshape(F, 2, 1, pairs_dev * BLOCK)
    returned = lax.all_to_all(
        adjoint_spec, ("fibre", "seg"), split_axis=0, concat_axis=2, tiled=True
    )
    returned = returned.reshape(freq_dev, 2, pair_total, BLOCK).astype(jnp.float32)
    adjoint_re, adjoint_im = (returned[:, 0], returned[:, 1])
    grad_first = jnp.stack(
        [
            adjoint_re * second_re - adjoint_im * second_im,
            adjoint_re * second_im + adjoint_im * second_re,
        ],
        axis=1,
    )
    grad_second = jnp.stack(
        [
            adjoint_re * first_re + adjoint_im * first_im,
            adjoint_re * first_im - adjoint_im * first_re,
        ],
        axis=1,
    )
    contributions = jnp.concatenate([grad_first, grad_second], axis=2)
    endpoint_ids = jnp.concatenate([slot_ids[:, 0], slot_ids[:, 1]])
    summed = jax.ops.segment_sum(
        jnp.moveaxis(contributions, 2, 0), endpoint_ids, num_segments=block_count
    )
    block_adjoint = jnp.moveaxis(summed, 0, 2).astype(jnp.bfloat16)
    outgoing = block_adjoint.reshape(freq_dev, 2, spread_count, CH_DEV)
    sources = synthesize(
        lax.all_to_all(outgoing, ("fibre", "seg"), split_axis=2, concat_axis=0, tiled=True), table
    )
    regrouped = lax.all_to_all(sources, "fibre", split_axis=0, concat_axis=1, tiled=True)
    return regrouped[None]


def angle_parts(freqs, times, scale):
    phase = (freqs[:, None].astype(np.int64) * times[None, :]) % S
    angles = phase.astype(np.float32) * np.float32(2.0 * np.pi / S)
    return np.stack([np.cos(angles) * scale, -np.sin(angles) * scale])


def band_tables(spread_count):
    order = np.concatenate([np.arange(0, F, 2), np.arange(1, F, 2)]).reshape(spread_count, -1)
    half = np.arange(S // 2)
    scale = np.float32(1.0) / np.sqrt(np.float32(S))
    forward = np.concatenate(
        [angle_parts(band, half, scale).reshape(-1, S // 2) for band in order]
    )
    backward = np.stack([forward[:F].T, forward[F:].T])
    shifts = (np.arange(LAGS) - LAGS // 2) % S
    lag_scale = np.float32(1.0) / np.sqrt(np.float32(F))
    lags = np.stack([angle_parts(band, shifts, lag_scale).reshape(-1, LAGS) for band in order])
    return [table.astype(jnp.bfloat16) for table in (forward, backward, lags)]


def dot(left, right, left_dim=1, right_dim=0):
    return lax.dot_general(
        left,
        right,
        (((left_dim,), (right_dim,)), ((), ())),
        preferred_element_type=jnp.float32,
    )


def fused_kernel(
    sizes, x_hbm, pairs, observed_hbm, mask_hbm, forward_hbm, backward_hbm, lags_hbm, out,
    x, observed, mask, forward, backward, lags, stage1, inbox1, signal, stage2, inbox2, picked, select, cross,
    stage_core, inbox_core, stage3, inbox3, inbox4, stage5, inbox5, stage6, inbox6, load_sem,
    core_sem, relay_send, relay_recv,
    send1, recv1, send2, recv2, send3, recv3, send4, recv4, send5, recv5, send6, recv6,
):
    fibres, segs, recs = sizes
    bands = fibres * segs
    g, f, s, r = (lax.axis_index(name) for name in ("groups", "fibre", "seg", "rec"))
    band = f * segs + s
    span, width = x.shape
    rows = span // 2
    chans = width // fibres
    freqs = F // bands
    low = jnp.bfloat16

    def at(fibre, seg, rec):
        return (g, fibre, seg, rec)

    def at_band(index):
        return at(index // segs, index % segs, r)

    def push(src, dst, send, recv, device):
        copy = pltpu.make_async_remote_copy(
            src_ref=src, dst_ref=dst, send_sem=send, recv_sem=recv,
            device_id=device, device_id_type=pl.DeviceIdType.MESH,
        )
        copy.start()
        return copy

    def arrived(dst, recv):
        pltpu.make_async_remote_copy(
            src_ref=dst, dst_ref=dst, send_sem=recv, recv_sem=recv,
            device_id=at(f, s, 1 - r), device_id_type=pl.DeviceIdType.MESH,
        ).wait_recv()

    def flipped(index, bits):
        result, bit = 0, 1
        while bit < bands:
            digit = index // bit % 2
            result += bit * (1 - digit if bits // bit % 2 else digit)
            bit *= 2
        return result

    partner = at(f, s, 1 - r)
    barrier = pltpu.get_barrier_semaphore()
    for d in range(1, bands):
        pl.semaphore_signal(
            barrier, inc=1, device_id=at_band(flipped(band, d)), device_id_type=pl.DeviceIdType.MESH
        )
    pl.semaphore_signal(barrier, inc=1, device_id=partner, device_id_type=pl.DeviceIdType.MESH)
    sends = []
    first_load = pltpu.make_async_copy(x_hbm, x, load_sem.at[0])
    first_load.start()
    loads = [
        pltpu.make_async_copy(forward_hbm, forward, load_sem.at[1]),
        pltpu.make_async_copy(lags_hbm.at[band], lags, load_sem.at[2]),
        pltpu.make_async_copy(observed_hbm.at[r], observed, load_sem.at[3]),
        pltpu.make_async_copy(mask_hbm, mask, load_sem.at[4]),
        pltpu.make_async_copy(backward_hbm, backward, load_sem.at[5]),
    ]
    first_load.wait()
    for load in loads:
        load.start()
    for j in range(fibres):
        part = x[:, j * chans : (j + 1) * chans]
        stage1[j] = jnp.concatenate([part[:rows], part[rows:]], axis=1)
    pl.semaphore_wait(barrier, bands)
    for d in range(fibres - 1, 0, -1):
        j = flipped(f, d)
        sends.append(push(stage1.at[j], inbox1.at[f], send1.at[d - 1], recv1.at[f], at(j, s, r)))
    inbox1[f] = stage1[f]

    total = select.shape[0]
    count = pairs.shape[1] * BLOCK
    lane = lax.broadcasted_iota(jnp.int32, (1, 2 * count), 1)
    target = lane
    for side in range(2):
        for n in range(pairs.shape[1]):
            first = side * count + n * BLOCK
            n = n % bands * recs + n // bands
            inside = (lane >= first) & (lane < first + BLOCK)
            target = jnp.where(inside, lane + (pairs[side, n] * BLOCK - first), target)
    row = lax.broadcasted_iota(jnp.int32, (total, 2 * count), 0)
    select[...] = jnp.where(row == target, 1.0, 0.0).astype(low)

    for d in range(1, fibres):
        k = (f + d) % fibres
        arrived(inbox1.at[k], recv1.at[k])
    for h in range(fibres // 2):
        early = inbox1[h].astype(jnp.float32)
        late = inbox1[h + fibres // 2].astype(jnp.float32)
        for parity, value in enumerate((early + late, early - late)):
            value = value.astype(low)
            base = parity * (S // 2) + h * span
            signal[base : base + rows] = value[:, :chans]
            signal[base + rows : base + span] = value[:, chans:]

    loads[0].wait()
    half = bands // 2
    for far in (1, 0):
        parity = flipped(f, far * (fibres // 2)) // (fibres // 2)
        top = pl.multiple_of(parity * F, F)
        held = signal[pl.ds(pl.multiple_of(parity * (S // 2), S // 2), S // 2), :]
        for pair in (1, 0):
            inner = flipped(f % 2, pair)
            start = pl.multiple_of(top + inner * (F // 2), F // 2)
            result = dot(forward[pl.ds(start, F // 2), :], held).astype(low)
            for i in range(segs):
                block = result[i * 2 * freqs : (i + 1) * 2 * freqs]
                stage2[parity * half + inner * segs + i] = jnp.concatenate(
                    [block[:freqs], block[freqs:]], axis=1
                )
            first = far * half + pair * segs
            for d in range(first + segs - 1, max(first - 1, 0), -1):
                j = flipped(band, d)
                sends.append(
                    push(stage2.at[j], inbox2.at[band], send2.at[d - 1], recv2.at[band], at_band(j))
                )
    inbox2[band] = stage2[band]
    for d in range(1, bands):
        k = (band + d) % bands
        arrived(inbox2.at[k], recv2.at[k])
    order = [fibre * segs + seg for seg in range(segs) for fibre in range(fibres)]
    spectra = jnp.concatenate(
        [
            jnp.concatenate([inbox2[k][:, p * chans : (p + 1) * chans] for k in order], axis=1)
            for p in range(2)
        ],
        axis=0,
    )
    picked[...] = dot(spectra, select[...])
    share = count // recs
    for h in range(recs):
        a0, a1, b0, b1 = (
            picked[p * freqs : (p + 1) * freqs, side * count + h * share : side * count + (h + 1) * share]
            for side in range(2)
            for p in range(2)
        )
        cross[h] = jnp.concatenate([a0 * b0 + a1 * b1, a1 * b0 - a0 * b1], axis=0).astype(low)
    loads[1].wait()
    stage_core[...] = dot(cross[1 - r], lags[...], 0, 0).astype(low)
    sends.append(push(stage_core, inbox_core, core_sem.at[0], core_sem.at[1], partner))
    partial = dot(cross[r], lags[...], 0, 0)
    arrived(inbox_core, core_sem.at[1])
    partial = (partial + inbox_core[...].astype(jnp.float32)).astype(low)
    stage3[...] = partial.reshape(stage3.shape)
    for d in range(bands - 1, 0, -1):
        j = flipped(band, d)
        sends.append(push(stage3.at[j], inbox3.at[band], send3.at[d - 1], recv3.at[band], at_band(j)))
    inbox3[band] = stage3[band]
    loads[2].wait()
    loads[3].wait()
    for d in range(1, bands):
        k = flipped(band, d)
        arrived(inbox3.at[k], recv3.at[k])
    synthetic = inbox3[0].astype(jnp.float32)
    for k in range(1, bands):
        synthetic += inbox3[k].astype(jnp.float32)
    window = mask[pl.ds(r, 1), :].astype(jnp.float32)
    inbox4[r, band] = (window * jnp.tanh(synthetic - observed[...])).astype(low)
    own = inbox4.at[r, band]
    for d in range(bands - 1, 0, -1):
        j = flipped(band, d)
        sends.append(push(own, own, send4.at[d - 1], recv4.at[band], at_band(j)))
    sends.append(push(own, own, relay_send.at[0], relay_recv.at[band], partner))
    for d in range(1, bands):
        k = flipped(band, d)
        arrived(inbox4.at[r, k], recv4.at[k])
        got = inbox4.at[r, k]
        sends.append(push(got, got, relay_send.at[d], relay_recv.at[k], partner))
    for d in range(bands):
        k = flipped(band, d)
        arrived(inbox4.at[1 - r, k], relay_recv.at[k])
    weights = inbox4[...].reshape(count, LAGS)
    adjoint = dot(lags[...], weights, 1, 1).astype(low).astype(jnp.float32)
    g0, g1 = (adjoint[:freqs], adjoint[freqs:])
    a0, a1 = (picked[:freqs, :count], picked[freqs:, :count])
    b0, b1 = (picked[:freqs, count:], picked[freqs:, count:])
    grads = jnp.concatenate(
        [
            jnp.concatenate([g0 * b0 - g1 * b1, g0 * a0 + g1 * a1], axis=1),
            jnp.concatenate([g0 * b1 + g1 * b0, g0 * a1 - g1 * a0], axis=1),
        ],
        axis=0,
    ).astype(low)
    summed = dot(grads, select[...], 1, 1).astype(low)
    for place, k in enumerate(order):
        cut = slice(place * chans, (place + 1) * chans)
        stage5[k] = jnp.concatenate([summed[:freqs, cut], summed[freqs:, cut]], axis=1)
    for d in range(bands - 1, 0, -1):
        j = flipped(band, d)
        sends.append(push(stage5.at[j], inbox5.at[band], send5.at[d - 1], recv5.at[band], at_band(j)))
    inbox5[band] = stage5[band]
    loads[4].wait()
    for d in range(1, bands):
        k = (band + d) % bands
        arrived(inbox5.at[k], recv5.at[k])
    held = []
    for parity in range(2):
        pieces = []
        for k in range(parity * bands // 2, (parity + 1) * bands // 2):
            pieces += [inbox5[k][:, :chans], inbox5[k][:, chans:]]
        held.append(jnp.concatenate(pieces, axis=0))
    for i in range(1, -1, -1):
        h = flipped(f, i) % 2
        cut = pl.ds(pl.multiple_of(h * span, span), span)
        even = dot(backward[0, cut, :], held[0])
        odd = dot(backward[1, cut, :], held[1])
        for late, value in enumerate((even + odd, even - odd)):
            value = value.astype(low)
            stage6[h + late * 2] = jnp.concatenate([value[:rows], value[rows:]], axis=1)
        for d in (2 + i, i):
            if d > 0:
                j = flipped(f, d)
                sends.append(push(stage6.at[j], inbox6.at[f], send6.at[d - 1], recv6.at[f], at(j, s, r)))
    inbox6[f] = stage6[f]
    for d in range(1, fibres):
        k = (f + d) % fibres
        arrived(inbox6.at[k], recv6.at[k])
    out[:rows, :] = jnp.concatenate([inbox6[k][:, :chans] for k in range(fibres)], axis=1)
    out[rows:, :] = jnp.concatenate([inbox6[k][:, chans:] for k in range(fibres)], axis=1)
    for copy in sends:
        copy.wait_send()


def fused_on_device(mesh_shape, tables, records, pairs, observed, lag_mask):
    fibres, segs, recs = (mesh_shape[name] for name in ("fibre", "seg", "rec"))
    bands = fibres * segs
    _, span, width = records.shape
    freqs = F // bands
    chans = width // fibres
    count = pairs.shape[0] * BLOCK
    low = jnp.bfloat16
    vmem = pl.BlockSpec(memory_space=pltpu.VMEM)
    hbm = pl.BlockSpec(memory_space=pltpu.HBM)
    row = (freqs, 2 * chans)
    slab = (span // 2, 2 * chans)
    corr = (BLOCK, LAGS)

    def sems(size):
        return [pltpu.SemaphoreType.DMA((size - 1,)), pltpu.SemaphoreType.DMA((size,))]

    result = pl.pallas_call(
        functools.partial(fused_kernel, (fibres, segs, recs)),
        out_shape=pltpu.VMEM((span, width), low),
        in_specs=[hbm, pl.BlockSpec(memory_space=pltpu.SMEM)] + [hbm] * 5,
        out_specs=vmem,
        scratch_shapes=[
            pltpu.VMEM((span, width), low),
            pltpu.VMEM(corr, jnp.float32),
            pltpu.VMEM(lag_mask.shape, jnp.int32),
            pltpu.VMEM((2 * F, S // 2), low),
            pltpu.VMEM((2, S // 2, F), low),
            pltpu.VMEM((2 * freqs, LAGS), low),
            pltpu.VMEM((fibres,) + slab, low),
            pltpu.VMEM((fibres,) + slab, low),
            pltpu.VMEM((S, chans), low),
            pltpu.VMEM((bands,) + row, low),
            pltpu.VMEM((bands,) + row, low),
            pltpu.VMEM((2 * freqs, 2 * count), jnp.float32),
            pltpu.VMEM((segs * width, 2 * count), low),
            pltpu.VMEM((recs, 2 * freqs, count // recs), low),
            pltpu.VMEM((count // recs, LAGS), low),
            pltpu.VMEM((count // recs, LAGS), low),
            pltpu.VMEM((bands,) + corr, low),
            pltpu.VMEM((bands,) + corr, low),
            pltpu.VMEM((recs, bands) + corr, low),
            pltpu.VMEM((bands,) + row, low),
            pltpu.VMEM((bands,) + row, low),
            pltpu.VMEM((fibres,) + slab, low),
            pltpu.VMEM((fibres,) + slab, low),
            pltpu.SemaphoreType.DMA((6,)),
            pltpu.SemaphoreType.DMA((2,)),
            pltpu.SemaphoreType.DMA((bands,)),
            pltpu.SemaphoreType.DMA((bands,)),
            *sems(fibres), *sems(bands), *sems(bands), *sems(bands), *sems(bands), *sems(fibres),
        ],
        compiler_params=pltpu.CompilerParams(
            has_side_effects=True, collective_id=0, vmem_limit_bytes=VMEM_GRANT
        ),
        name="adjoint",
    )(records[0], pairs.T, observed, lag_mask, *tables)
    return result[None]


def fits_fused(shape, records, pairs):
    fibres, segs, recs = (shape[name] for name in ("fibre", "seg", "rec"))
    chans = records.shape[2] // (shape["groups"] * segs * fibres)
    return (
        fibres == 4
        and recs == 2
        and segs & (segs - 1) == 0
        and 2 * chans == 128
        and pairs.shape[0] == fibres * segs * recs
        and F // (fibres * segs) >= 16
    )


def solution(mesh):
    in_specs = (
        P("rec", "fibre", ("groups", "seg")),
        P(),
        P(("groups", "fibre", "seg"), None, None),
        P(("groups", "fibre", "seg"), None),
    )
    out_specs = P("rec", "fibre", ("groups", "seg"))
    shape = dict(mesh.shape)

    def run(records, pairs, observed, lag_mask):
        args = (records, pairs, observed, lag_mask)
        if not fits_fused(shape, records, pairs):
            return jax.shard_map(
                on_device, mesh=mesh, in_specs=in_specs, out_specs=out_specs, check_vma=False
            )(*args)
        tables = [jnp.asarray(t) for t in band_tables(shape["fibre"] * shape["seg"])]

        def body(*blocks):
            return fused_on_device(shape, tables, *blocks)

        return jax.shard_map(
            body, mesh=mesh, in_specs=in_specs, out_specs=out_specs, check_vma=False
        )(*args)

    return run
```

profile of v0, /device:TPU:0, one launch (start us, length us, event | category | flops | bytes accessed | tf_op | source)
XLA Modules:
  0.0 50.3 jit_solution(14506531878814779484)
XLA Ops:
  0.0 49.5 %adjoint.1 = bf16[512,256]{1,0:T(8,128)(2,1)S(1)} custom-call(bf16[512,256]{1,0:T(8,128)(2,1)} %bitcast.4, s32[2,16]{1,0:T(2,128)} %bitcast.5, f32[2,32,256]{2,1,0:T(8,128)} %observed_hbm.1, s32[2,256]{1,0:T(2,128)} %mask_hbm.1, bf16[2048,1024]{1,0:T(8,128)(2,1)} %constant.6.clone.forward_hbm, bf16[2,1024,1024]{2,1,0:T(8,128)(2,1)} %constant.7.clone.backward_hbm, ...), custom_call_target="tpu_custom_call" | custom-call | tf_op jit(solution)/shard_map/adjoint/pallas_call | solution.py:411
  49.5 0.7 %copy.9 = bf16[1,512,256]{2,1,0:T(8,128)(2,1)} copy(bf16[1,512,256]{2,1,0:T(8,128)(2,1)S(1)} %bitcast.3) | data formatting | bytes 524288
where the time goes:
time: 50.4 us; the launch traced here: 50.3 us
  Pallas kernels  49.5 us (98%)
  local copies, waits for them, and re-layouts  0.71 us (1%)
    pallas_call x1, Pallas kernels, fused_on_device(): pl.pallas_call(functools.partial(fused_kernel, (fibres, segs, recs)), out...  49.5 us

commit v1 on v0

v1 whole, which is shorter than its diff:
```python
import functools

import jax
import jax.numpy as jnp
import numpy as np
from jax import lax
from jax.experimental import pallas as pl
from jax.experimental.pallas import tpu as pltpu
from jax.sharding import PartitionSpec as P

S = 2048
F = 1024
LAGS = 256
BLOCK = 32
CH_DEV = 64
VMEM_GRANT = 60899328


def forward_table():
    freq_index = jnp.arange(F, dtype=jnp.int32)
    time_index = jnp.arange(S, dtype=jnp.int32)
    phase = freq_index[:, None] * time_index[None, :] % S
    angles = phase.astype(jnp.float32) * (2.0 * jnp.pi / S)
    scale = 1.0 / jnp.sqrt(jnp.float32(S))
    return jnp.stack(
        [
            (jnp.cos(angles) * scale).astype(jnp.bfloat16),
            (-jnp.sin(angles) * scale).astype(jnp.bfloat16),
        ],
        axis=1,
    )


def lag_table():
    freq_index = jnp.arange(F, dtype=jnp.int32)
    shifts = (jnp.arange(LAGS, dtype=jnp.int32) - LAGS // 2) % S
    phase = freq_index[:, None] * shifts[None, :] % S
    angles = phase.astype(jnp.float32) * (2.0 * jnp.pi / S)
    scale = 1.0 / jnp.sqrt(jnp.float32(F))
    return jnp.stack(
        [
            (jnp.cos(angles) * scale).astype(jnp.bfloat16),
            (-jnp.sin(angles) * scale).astype(jnp.bfloat16),
        ],
        axis=1,
    )


def synthesize(incoming, table):
    count = incoming.shape[-1]
    flat = incoming.reshape(2 * F, count)
    result = jnp.einsum(
        "qn,qt->tn", flat, table.reshape(2 * F, S), preferred_element_type=jnp.float32
    )
    return result.astype(jnp.bfloat16)


def on_device(records, pairs, observed, lag_mask):
    fibre_count = lax.axis_size("fibre")
    seg_count = lax.axis_size("seg")
    spread_count = fibre_count * seg_count
    freq_dev = F // spread_count
    blocks_dev = CH_DEV // BLOCK
    block_count = CH_DEV * spread_count // BLOCK
    pair_total = pairs.shape[0]
    pairs_dev = pair_total // spread_count
    table = forward_table()
    lags = lag_table()
    spans = records.reshape(1, S // fibre_count, fibre_count, CH_DEV)
    incoming = lax.all_to_all(spans, "fibre", split_axis=2, concat_axis=1, tiled=True)
    count = incoming.shape[3]
    signal = incoming.reshape(S, count)
    result = jnp.einsum(
        "qs,sn->qn", table.reshape(2 * F, S), signal, preferred_element_type=jnp.float32
    )
    spectra = result.reshape(F, 2, count).astype(jnp.bfloat16)
    widened = lax.all_to_all(spectra, ("fibre", "seg"), split_axis=0, concat_axis=2, tiled=True)
    seg_blocks = fibre_count * blocks_dev
    slot_ids = (
        pairs % seg_blocks // blocks_dev * seg_count + pairs // seg_blocks
    ) * blocks_dev + pairs % blocks_dev
    blocks_grid = widened.reshape(freq_dev, 2, block_count, BLOCK)
    first_side = jnp.take(blocks_grid, slot_ids[:, 0], axis=2).astype(jnp.float32)
    second_side = jnp.take(blocks_grid, slot_ids[:, 1], axis=2).astype(jnp.float32)
    first_re, first_im = (first_side[:, 0], first_side[:, 1])
    second_re, second_im = (second_side[:, 0], second_side[:, 1])
    cross_re = first_re * second_re + first_im * second_im
    cross_im = first_im * second_re - first_re * second_im
    cross_spec = jnp.stack([cross_re, cross_im], axis=1).astype(jnp.bfloat16)
    cross_spec = cross_spec.reshape(freq_dev, 2, spread_count, pairs_dev * BLOCK)
    owned_spec = lax.all_to_all(
        cross_spec, ("fibre", "seg"), split_axis=2, concat_axis=0, tiled=True
    )
    owned_spec = owned_spec.reshape(F, 2, pairs_dev * BLOCK)
    partial_corr = jnp.einsum("wpx,wpl->xl", owned_spec, lags, preferred_element_type=jnp.float32)
    synthetic = (
        lax.psum(partial_corr.astype(jnp.bfloat16), "rec")
        .astype(jnp.float32)
        .reshape(pairs_dev, BLOCK, LAGS)
    )
    weights = lag_mask[:, None, :].astype(jnp.float32) * jnp.tanh(synthetic - observed)
    weights_low = weights.astype(jnp.bfloat16).reshape(pairs_dev * BLOCK, LAGS)
    adjoint_spec = jnp.einsum("xl,wpl->wpx", weights_low, lags, preferred_element_type=jnp.float32)
    adjoint_spec = adjoint_spec.astype(jnp.bfloat16).reshape(F, 2, 1, pairs_dev * BLOCK)
    returned = lax.all_to_all(
        adjoint_spec, ("fibre", "seg"), split_axis=0, concat_axis=2, tiled=True
    )
    returned = returned.reshape(freq_dev, 2, pair_total, BLOCK).astype(jnp.float32)
    adjoint_re, adjoint_im = (returned[:, 0], returned[:, 1])
    grad_first = jnp.stack(
        [
            adjoint_re * second_re - adjoint_im * second_im,
            adjoint_re * second_im + adjoint_im * second_re,
        ],
        axis=1,
    )
    grad_second = jnp.stack(
        [
            adjoint_re * first_re + adjoint_im * first_im,
            adjoint_re * first_im - adjoint_im * first_re,
        ],
        axis=1,
    )
    contributions = jnp.concatenate([grad_first, grad_second], axis=2)
    endpoint_ids = jnp.concatenate([slot_ids[:, 0], slot_ids[:, 1]])
    summed = jax.ops.segment_sum(
        jnp.moveaxis(contributions, 2, 0), endpoint_ids, num_segments=block_count
    )
    block_adjoint = jnp.moveaxis(summed, 0, 2).astype(jnp.bfloat16)
    outgoing = block_adjoint.reshape(freq_dev, 2, spread_count, CH_DEV)
    sources = synthesize(
        lax.all_to_all(outgoing, ("fibre", "seg"), split_axis=2, concat_axis=0, tiled=True), table
    )
    regrouped = lax.all_to_all(sources, "fibre", split_axis=0, concat_axis=1, tiled=True)
    return regrouped[None]


def window_tables(bands, segs):
    span, reach, n = S // bands, LAGS // 2, S // bands + LAGS
    half = n // 2

    def parts(freqs, times):
        angles = (freqs * times % n) * (2.0 * np.pi / n)
        return np.cos(angles), -np.sin(angles)

    freqs, places = np.arange(half), np.arange(n)
    shifts = np.arange(LAGS) - reach
    ends = np.where(freqs == 0, 1.0, 2.0) / (n * 2.0 * np.sqrt(F))

    def table(times, scale):
        real, imag = parts(freqs[None, :], times[:, None])
        imag[:, 0] = np.where(times % 2 == 0, 1.0, -1.0)
        return np.concatenate([real * scale, imag * scale], axis=1)

    whole = table(places, np.ones(half))
    core = whole[reach : reach + span]
    left, right = whole[:reach], whole[reach + span :]
    halo = np.stack([np.concatenate(p) for p in ((right, left), (left, right))])
    lags = table(shifts, ends).T
    taps = table(shifts, np.ones(half))
    back = table(places[reach : reach + span], ends)
    return [t.astype(np.float32).astype(jnp.bfloat16) for t in (core, halo, lags, taps, back)]


def dot(left, right, left_dim=1, right_dim=0):
    return lax.dot_general(
        left,
        right,
        (((left_dim,), (right_dim,)), ((), ())),
        preferred_element_type=jnp.float32,
    )


def spectral_product(p, q, sign):
    p0, p1 = p
    q0, q1 = q
    ends = lax.broadcasted_iota(jnp.int32, p0.shape, 1) == 0
    both = p1 * q1
    real = p0 * q0 + jnp.where(ends, 0.0, sign * both)
    imag = jnp.where(ends, both, p1 * q0 - sign * (p0 * q1))
    return real, imag


def fused_kernel(
    sizes, x_hbm, pairs, observed_hbm, mask_hbm, core_hbm, halo_hbm, lags_hbm, taps_hbm, back_hbm, out,
    core, halo, rest, observed, mask, core_table, halo_table, lags, taps, back,
    stage_sum, inbox_sum, partial_spec, core_spec, full_spec, select, cross,
    stage_core, inbox_core, stage3, inbox3, inbox4, grads, stage6,
    load_sem, send1, recv1, send2, recv2, core_sem, relay_send, relay_recv,
    send3, recv3, send4, recv4, send6, recv6,
):
    fibres, segs, recs = sizes
    bands = fibres * segs
    g, f, s, r = (lax.axis_index(name) for name in ("groups", "fibre", "seg", "rec"))
    o = 1 - s
    band = f * segs + s
    span, reach, width = S // bands, LAGS // 2, x_hbm.shape[1]
    n = span + LAGS
    half = n // 2
    blocks = width // BLOCK
    low, full = jnp.bfloat16, jnp.float32

    def at(fibre, seg, rec):
        return (g, fibre, seg, rec)

    def at_band(index):
        return at(index // segs, index % segs, r)

    def push(src, dst, send, recv, device):
        copy = pltpu.make_async_remote_copy(
            src_ref=src, dst_ref=dst, send_sem=send, recv_sem=recv,
            device_id=device, device_id_type=pl.DeviceIdType.MESH,
        )
        copy.start()
        return copy

    def arrived(dst, recv):
        pltpu.make_async_remote_copy(
            src_ref=dst, dst_ref=dst, send_sem=recv, recv_sem=recv,
            device_id=at(f, s, 1 - r), device_id_type=pl.DeviceIdType.MESH,
        ).wait_recv()

    def rows(start, count, unit):
        return pl.ds(pl.multiple_of(start, unit), count)

    def flipped(index, bits):
        result, bit = 0, 1
        while bit < bands:
            digit = index // bit % 2
            result += bit * (1 - digit if bits // bit % 2 else digit)
            bit *= 2
        return result

    partner = at(f, s, 1 - r)
    across = at(f, o, r)
    barrier = pltpu.get_barrier_semaphore()
    for d in range(1, bands):
        pl.semaphore_signal(
            barrier, inc=1, device_id=at_band(flipped(band, d)), device_id_type=pl.DeviceIdType.MESH
        )
    pl.semaphore_signal(barrier, inc=1, device_id=partner, device_id_type=pl.DeviceIdType.MESH)
    locals_ = [
        pltpu.make_async_copy(x_hbm.at[rows(span * s, span, reach)], core.at[s], load_sem.at[0]),
        pltpu.make_async_copy(
            x_hbm.at[rows(span - reach * s, reach, reach)], halo.at[s, pl.ds(0, reach)], load_sem.at[1]
        ),
        pltpu.make_async_copy(x_hbm.at[rows((2 * span - reach) * o, reach, reach)], rest, load_sem.at[2]),
    ]
    loads = [
        pltpu.make_async_copy(core_hbm, core_table, load_sem.at[3]),
        pltpu.make_async_copy(halo_hbm.at[s], halo_table, load_sem.at[4]),
        pltpu.make_async_copy(lags_hbm, lags, load_sem.at[5]),
        pltpu.make_async_copy(observed_hbm.at[r], observed, load_sem.at[6]),
        pltpu.make_async_copy(mask_hbm, mask, load_sem.at[7]),
        pltpu.make_async_copy(taps_hbm, taps, load_sem.at[8]),
        pltpu.make_async_copy(back_hbm, back, load_sem.at[9]),
    ]
    for load in locals_ + loads:
        load.start()
    pl.semaphore_wait(barrier, bands)
    tail = pl.ds(reach, reach)
    after, before = at((f + 1) % fibres, 0, r), at((f + fibres - 1) % fibres, 1, r)
    sends = [
        push(x_hbm.at[pl.ds(2 * span - reach, reach)], halo.at[s, tail], send1.at[2], recv1.at[2 + s], after),
        push(x_hbm.at[pl.ds(0, reach)], halo.at[s, tail], send1.at[3], recv1.at[2 + s], before),
        push(x_hbm.at[rows(span * o, span, reach)], core.at[s], send1.at[0], recv1.at[0], across),
        push(
            x_hbm.at[rows(span - reach * o, reach, reach)], halo.at[s, pl.ds(0, reach)],
            send1.at[1], recv1.at[1], across,
        ),
    ]
    for load in locals_:
        load.wait()
    folded = sum(
        part.astype(full).reshape(-1, 8, width).sum(axis=0)
        for part in (core[s], halo[s, pl.ds(0, reach)], rest[...])
    )
    odd = lax.broadcasted_iota(jnp.int32, folded.shape, 0) % 2 == 1
    stage_sum[...] = jnp.concatenate(
        [
            jnp.sum(folded, axis=0, keepdims=True),
            jnp.sum(jnp.where(odd, -folded, folded), axis=0, keepdims=True),
        ],
        axis=0,
    )
    for d in range(bands - 1, 0, -1):
        j = flipped(band, d)
        sends.append(push(stage_sum, inbox_sum.at[band], send2.at[d - 1], recv2.at[band], at_band(j)))
    inbox_sum[band] = stage_sum[...]

    count = pairs.shape[1] * BLOCK
    slots = [j * recs + h for h in range(recs) for j in range(bands)]
    lane = lax.broadcasted_iota(jnp.int32, (1, 2 * count), 1)
    target = lane
    for side in range(2):
        for place, pair in enumerate(slots):
            first = side * count + place * BLOCK
            inside = (lane >= first) & (lane < first + BLOCK)
            target = jnp.where(inside, lane + (pairs[side, pair] * BLOCK - first), target)
    row = lax.broadcasted_iota(jnp.int32, select.shape, 0)
    select[...] = jnp.where(row == target, 1.0, 0.0).astype(low)

    def core_part(seg):
        part = dot(core[seg], core_table[...], 0, 0)
        partial_spec[seg] = part
        core_spec[rows(seg * blocks, blocks, blocks)] = part.astype(low).reshape(blocks, BLOCK, n)

    loads[0].wait()
    core_part(s)
    arrived(core.at[o], recv1.at[0])
    core_part(o)
    for d in range(1, bands):
        k = (band + d) % bands
        arrived(inbox_sum.at[k], recv2.at[k])
    loads[1].wait()
    arrived(halo.at[s, tail], recv1.at[2 + s])
    arrived(halo.at[o, tail], recv1.at[2 + o])
    arrived(halo.at[o, pl.ds(0, reach)], recv1.at[1])
    for seg in range(segs):
        part = partial_spec[seg] + dot(halo[seg], halo_table[...], 0, 0)
        total = sum(inbox_sum[k * segs + seg] for k in range(fibres)) * (n / S)
        total = jnp.concatenate([total] * 4, axis=0).T
        head = lax.broadcasted_iota(jnp.int32, (1, 128), 1) == 0
        part = jnp.concatenate(
            [
                part[:, :128] + jnp.where(head, total[:, 0:1], 0.0),
                part[:, 128:half],
                part[:, half : half + 128] - jnp.where(head, total[:, 1:2], 0.0),
                part[:, half + 128 :],
            ],
            axis=1,
        )
        full_spec[pl.ds(seg * blocks, blocks)] = part.astype(low).reshape(blocks, BLOCK, n)

    def block(spec, index):
        value = spec[index].astype(full)
        return value[:, :half], value[:, half:]

    def correlate(place, h):
        for j in range(bands):
            pair = j * recs + h
            first = block(full_spec, pairs[0, pair])
            second = block(core_spec, pairs[1, pair])
            here = pl.ds(j * BLOCK, BLOCK)
            real, imag = spectral_product(first, second, 1.0)
            cross[place, here, pl.ds(0, half)] = real.astype(low)
            cross[place, here, pl.ds(half, half)] = imag.astype(low)
        return dot(cross[place], lags[...])

    loads[2].wait()
    stage_core[...] = correlate(0, 1 - r).astype(low)
    sends.append(push(stage_core, inbox_core, core_sem.at[0], core_sem.at[1], partner))
    partial = correlate(1, r)
    arrived(inbox_core, core_sem.at[1])
    partial = (partial + inbox_core[...].astype(full)).astype(low)
    stage3[...] = partial.reshape(stage3.shape)
    for d in range(bands - 1, 0, -1):
        j = flipped(band, d)
        sends.append(push(stage3.at[j], inbox3.at[band], send3.at[d - 1], recv3.at[band], at_band(j)))
    inbox3[band] = stage3[band]
    loads[3].wait()
    loads[4].wait()
    for d in range(1, bands):
        k = flipped(band, d)
        arrived(inbox3.at[k], recv3.at[k])
    synthetic = inbox3[0].astype(full)
    for k in range(1, bands):
        synthetic += inbox3[k].astype(full)
    window = mask[pl.ds(r, 1), :].astype(full)
    inbox4[r, band] = (window * jnp.tanh(synthetic - observed[...])).astype(low)
    own = inbox4.at[r, band]
    for d in range(bands - 1, 0, -1):
        j = flipped(band, d)
        sends.append(push(own, own, send4.at[d - 1], recv4.at[band], at_band(j)))
    sends.append(push(own, own, relay_send.at[0], relay_recv.at[band], partner))
    for d in range(1, bands):
        k = flipped(band, d)
        arrived(inbox4.at[r, k], recv4.at[k])
        got = inbox4.at[r, k]
        sends.append(push(got, got, relay_send.at[d], relay_recv.at[k], partner))
    for d in range(bands):
        k = flipped(band, d)
        arrived(inbox4.at[1 - r, k], relay_recv.at[k])
    loads[5].wait()
    for h in range(recs):
        spread = dot(inbox4[h].reshape(bands * BLOCK, LAGS), taps[...])
        for j in range(bands):
            pair = j * recs + h
            filters = spread[j * BLOCK : (j + 1) * BLOCK]
            filters = filters[:, :half], filters[:, half:]
            first = block(full_spec, pairs[0, pair])
            second = block(full_spec, pairs[1, pair])
            place = (h * bands + j) * BLOCK
            for base, parts in (
                (place, spectral_product(filters, second, -1.0)),
                (count + place, spectral_product(first, filters, 1.0)),
            ):
                for p in range(2):
                    grads[pl.ds(base, BLOCK), pl.ds(p * half, half)] = parts[p].astype(low)
    loads[6].wait()

    def source(seg):
        summed = dot(select[rows(seg * width, width, width), :], grads[...]).astype(low)
        return dot(back[...], summed, 1, 1).astype(low)

    here = rows(span * s, span, span)
    stage6[...] = source(o)
    sends.append(push(stage6, out.at[here, :], send6.at[0], recv6.at[0], across))
    out[here, :] = source(s)
    there = rows(span * o, span, span)
    arrived(out.at[there, :], recv6.at[0])
    for copy in sends:
        copy.wait_send()


def fused_on_device(mesh_shape, tables, records, pairs, observed, lag_mask):
    fibres, segs, recs = (mesh_shape[name] for name in ("fibre", "seg", "rec"))
    bands = fibres * segs
    _, extent, width = records.shape
    span, reach = S // bands, LAGS // 2
    n = span + LAGS
    count = pairs.shape[0] * BLOCK
    own = count // recs
    low, full = jnp.bfloat16, jnp.float32
    vmem = pl.BlockSpec(memory_space=pltpu.VMEM)
    hbm = pl.BlockSpec(memory_space=pltpu.HBM)
    corr = (BLOCK, LAGS)

    def sems(*sizes):
        return [pltpu.SemaphoreType.DMA((size,)) for size in sizes]

    result = pl.pallas_call(
        functools.partial(fused_kernel, (fibres, segs, recs)),
        out_shape=pltpu.VMEM((extent, width), low),
        in_specs=[hbm, pl.BlockSpec(memory_space=pltpu.SMEM)] + [hbm] * 7,
        out_specs=vmem,
        scratch_shapes=[
            pltpu.VMEM((segs, span, width), low),
            pltpu.VMEM((segs, 2 * reach, width), low),
            pltpu.VMEM((reach, width), low),
            pltpu.VMEM(corr, full),
            pltpu.VMEM(lag_mask.shape, jnp.int32),
            pltpu.VMEM((span, n), low),
            pltpu.VMEM((2 * reach, n), low),
            pltpu.VMEM((n, LAGS), low),
            pltpu.VMEM((LAGS, n), low),
            pltpu.VMEM((span, n), low),
            pltpu.VMEM((2, width), full),
            pltpu.VMEM((bands, 2, width), full),
            pltpu.VMEM((segs, width, n), full),
            pltpu.VMEM((segs * width // BLOCK, BLOCK, n), low),
            pltpu.VMEM((segs * width // BLOCK, BLOCK, n), low),
            pltpu.VMEM((segs * width, 2 * count), low),
            pltpu.VMEM((recs, own, n), low),
            pltpu.VMEM((own, LAGS), low),
            pltpu.VMEM((own, LAGS), low),
            pltpu.VMEM((bands,) + corr, low),
            pltpu.VMEM((bands,) + corr, low),
            pltpu.VMEM((recs, bands) + corr, low),
            pltpu.VMEM((2 * count, n), low),
            pltpu.VMEM((span, width), low),
            *sems(10, 4, 4, bands - 1, bands, 2, bands, bands),
            *sems(bands - 1, bands, bands - 1, bands, 1, 1),
        ],
        compiler_params=pltpu.CompilerParams(
            has_side_effects=True, collective_id=0, vmem_limit_bytes=VMEM_GRANT
        ),
        name="adjoint",
    )(records[0], pairs.T, observed, lag_mask, *tables)
    return result[None]


def fits_fused(shape, records, pairs):
    fibres, segs, recs = (shape[name] for name in ("fibre", "seg", "rec"))
    bands = fibres * segs
    width = records.shape[2] // (shape["groups"] * segs)
    return (
        fibres > 1
        and fibres & (fibres - 1) == 0
        and segs == 2
        and recs == 2
        and width % 128 == 0
        and width * segs <= 512
        and S // bands >= LAGS
        and pairs.shape[0] == bands * recs
    )


def solution(mesh):
    in_specs = (
        P("rec", "fibre", ("groups", "seg")),
        P(),
        P(("groups", "fibre", "seg"), None, None),
        P(("groups", "fibre", "seg"), None),
    )
    out_specs = P("rec", "fibre", ("groups", "seg"))
    shape = dict(mesh.shape)

    def run(records, pairs, observed, lag_mask):
        args = (records, pairs, observed, lag_mask)
        if not fits_fused(shape, records, pairs):
            return jax.shard_map(
                on_device, mesh=mesh, in_specs=in_specs, out_specs=out_specs, check_vma=False
            )(*args)
        tables = [jnp.asarray(t) for t in window_tables(shape["fibre"] * shape["seg"], shape["seg"])]

        def body(*blocks):
            return fused_on_device(shape, tables, *blocks)

        return jax.shard_map(
            body, mesh=mesh, in_specs=in_specs, out_specs=out_specs, check_vma=False
        )(*args)

    return run
```

time: 50.4 us -> 34.3 us (0.68)
  Pallas kernels: 49.5 us -> 33.4 us
    pallas_call x1, Pallas kernels: 49.5 us -> 33.4 us  [fused_on_device(): pl.pallas_call(functools.partial(fused_kernel, (fibres, segs, recs)), out...]
where the time goes in v1:
time: 34.3 us; the launch traced here: 34.1 us
  Pallas kernels  33.4 us (97%)
  local copies, waits for them, and re-layouts  0.71 us (2%)
    pallas_call x1, Pallas kernels, fused_on_device(): pl.pallas_call(functools.partial(fused_kernel, (fibres, segs, recs)), out...  33.4 us
    unnamed x1, local copies, waits for them, and re-layouts  0.71 us

profile of v1, /device:TPU:0, one launch (start us, length us, event | category | flops | bytes accessed | tf_op | source)
XLA Modules:
  0.0 34.1 jit_solution(5580020707966354412)
XLA Ops:
  0.0 33.4 %adjoint.1 = bf16[512,256]{1,0:T(8,128)(2,1)S(1)} custom-call(bf16[512,256]{1,0:T(8,128)(2,1)} %bitcast.4, s32[2,16]{1,0:T(2,128)} %bitcast.5, f32[2,32,256]{2,1,0:T(8,128)} %observed_hbm.1, s32[2,256]{1,0:T(2,128)} %mask_hbm.1, bf16[256,512]{1,0:T(8,128)(2,1)} %constant.10.clone.core_hbm, bf16[2,256,512]{2,1,0:T(8,128)(2,1)} %constant.11.clone.halo_hbm, ...), custom_call_target="tpu_custom_call" | custom-call | tf_op jit(solution)/shard_map/adjoint/pallas_call | solution.py:432
  33.4 0.7 %copy.11 = bf16[1,512,256]{2,1,0:T(8,128)(2,1)} copy(bf16[1,512,256]{2,1,0:T(8,128)(2,1)S(1)} %bitcast.3) | data formatting | bytes 524288

commit v2 on v1

v2 whole, which is shorter than its diff:
```python
import functools

import jax
import jax.numpy as jnp
import numpy as np
from jax import lax
from jax.experimental import pallas as pl
from jax.experimental.pallas import tpu as pltpu
from jax.sharding import PartitionSpec as P

S = 2048
F = 1024
LAGS = 256
BLOCK = 32
CH_DEV = 64
VMEM_GRANT = 60899328


def forward_table():
    freq_index = jnp.arange(F, dtype=jnp.int32)
    time_index = jnp.arange(S, dtype=jnp.int32)
    phase = freq_index[:, None] * time_index[None, :] % S
    angles = phase.astype(jnp.float32) * (2.0 * jnp.pi / S)
    scale = 1.0 / jnp.sqrt(jnp.float32(S))
    return jnp.stack(
        [
            (jnp.cos(angles) * scale).astype(jnp.bfloat16),
            (-jnp.sin(angles) * scale).astype(jnp.bfloat16),
        ],
        axis=1,
    )


def lag_table():
    freq_index = jnp.arange(F, dtype=jnp.int32)
    shifts = (jnp.arange(LAGS, dtype=jnp.int32) - LAGS // 2) % S
    phase = freq_index[:, None] * shifts[None, :] % S
    angles = phase.astype(jnp.float32) * (2.0 * jnp.pi / S)
    scale = 1.0 / jnp.sqrt(jnp.float32(F))
    return jnp.stack(
        [
            (jnp.cos(angles) * scale).astype(jnp.bfloat16),
            (-jnp.sin(angles) * scale).astype(jnp.bfloat16),
        ],
        axis=1,
    )


def synthesize(incoming, table):
    count = incoming.shape[-1]
    flat = incoming.reshape(2 * F, count)
    result = jnp.einsum(
        "qn,qt->tn", flat, table.reshape(2 * F, S), preferred_element_type=jnp.float32
    )
    return result.astype(jnp.bfloat16)


def on_device(records, pairs, observed, lag_mask):
    fibre_count = lax.axis_size("fibre")
    seg_count = lax.axis_size("seg")
    spread_count = fibre_count * seg_count
    freq_dev = F // spread_count
    blocks_dev = CH_DEV // BLOCK
    block_count = CH_DEV * spread_count // BLOCK
    pair_total = pairs.shape[0]
    pairs_dev = pair_total // spread_count
    table = forward_table()
    lags = lag_table()
    spans = records.reshape(1, S // fibre_count, fibre_count, CH_DEV)
    incoming = lax.all_to_all(spans, "fibre", split_axis=2, concat_axis=1, tiled=True)
    count = incoming.shape[3]
    signal = incoming.reshape(S, count)
    result = jnp.einsum(
        "qs,sn->qn", table.reshape(2 * F, S), signal, preferred_element_type=jnp.float32
    )
    spectra = result.reshape(F, 2, count).astype(jnp.bfloat16)
    widened = lax.all_to_all(spectra, ("fibre", "seg"), split_axis=0, concat_axis=2, tiled=True)
    seg_blocks = fibre_count * blocks_dev
    slot_ids = (
        pairs % seg_blocks // blocks_dev * seg_count + pairs // seg_blocks
    ) * blocks_dev + pairs % blocks_dev
    blocks_grid = widened.reshape(freq_dev, 2, block_count, BLOCK)
    first_side = jnp.take(blocks_grid, slot_ids[:, 0], axis=2).astype(jnp.float32)
    second_side = jnp.take(blocks_grid, slot_ids[:, 1], axis=2).astype(jnp.float32)
    first_re, first_im = (first_side[:, 0], first_side[:, 1])
    second_re, second_im = (second_side[:, 0], second_side[:, 1])
    cross_re = first_re * second_re + first_im * second_im
    cross_im = first_im * second_re - first_re * second_im
    cross_spec = jnp.stack([cross_re, cross_im], axis=1).astype(jnp.bfloat16)
    cross_spec = cross_spec.reshape(freq_dev, 2, spread_count, pairs_dev * BLOCK)
    owned_spec = lax.all_to_all(
        cross_spec, ("fibre", "seg"), split_axis=2, concat_axis=0, tiled=True
    )
    owned_spec = owned_spec.reshape(F, 2, pairs_dev * BLOCK)
    partial_corr = jnp.einsum("wpx,wpl->xl", owned_spec, lags, preferred_element_type=jnp.float32)
    synthetic = (
        lax.psum(partial_corr.astype(jnp.bfloat16), "rec")
        .astype(jnp.float32)
        .reshape(pairs_dev, BLOCK, LAGS)
    )
    weights = lag_mask[:, None, :].astype(jnp.float32) * jnp.tanh(synthetic - observed)
    weights_low = weights.astype(jnp.bfloat16).reshape(pairs_dev * BLOCK, LAGS)
    adjoint_spec = jnp.einsum("xl,wpl->wpx", weights_low, lags, preferred_element_type=jnp.float32)
    adjoint_spec = adjoint_spec.astype(jnp.bfloat16).reshape(F, 2, 1, pairs_dev * BLOCK)
    returned = lax.all_to_all(
        adjoint_spec, ("fibre", "seg"), split_axis=0, concat_axis=2, tiled=True
    )
    returned = returned.reshape(freq_dev, 2, pair_total, BLOCK).astype(jnp.float32)
    adjoint_re, adjoint_im = (returned[:, 0], returned[:, 1])
    grad_first = jnp.stack(
        [
            adjoint_re * second_re - adjoint_im * second_im,
            adjoint_re * second_im + adjoint_im * second_re,
        ],
        axis=1,
    )
    grad_second = jnp.stack(
        [
            adjoint_re * first_re + adjoint_im * first_im,
            adjoint_re * first_im - adjoint_im * first_re,
        ],
        axis=1,
    )
    contributions = jnp.concatenate([grad_first, grad_second], axis=2)
    endpoint_ids = jnp.concatenate([slot_ids[:, 0], slot_ids[:, 1]])
    summed = jax.ops.segment_sum(
        jnp.moveaxis(contributions, 2, 0), endpoint_ids, num_segments=block_count
    )
    block_adjoint = jnp.moveaxis(summed, 0, 2).astype(jnp.bfloat16)
    outgoing = block_adjoint.reshape(freq_dev, 2, spread_count, CH_DEV)
    sources = synthesize(
        lax.all_to_all(outgoing, ("fibre", "seg"), split_axis=2, concat_axis=0, tiled=True), table
    )
    regrouped = lax.all_to_all(sources, "fibre", split_axis=0, concat_axis=1, tiled=True)
    return regrouped[None]


def window_tables(bands):
    span, reach, n = S // bands, LAGS // 2, S // bands + LAGS
    half = n // 2
    freqs, places = np.arange(half), np.arange(n)
    shifts = np.arange(LAGS) - reach
    ends = np.where(freqs == 0, 1.0, 2.0) / (n * 2.0 * np.sqrt(F))

    def table(times, scale):
        angles = (freqs[None, :] * times[:, None] % n) * (2.0 * np.pi / n)
        real, imag = np.cos(angles), -np.sin(angles)
        imag[:, 0] = np.where(times % 2 == 0, 1.0, -1.0)
        return np.concatenate([real * scale, imag * scale], axis=1)

    whole = table(places, np.ones(half))
    left, core, right = whole[:reach], whole[reach : reach + span], whole[reach + span :]
    signs = np.where(places % 2 == 0, 1.0, -1.0)[:, None]
    parts = (slice(reach, reach + span), slice(0, reach), slice(0, n), slice(0, 0))
    fixes = np.stack([row for p in parts for row in (whole[p].sum(0), -(signs * whole)[p].sum(0))]) / S
    lags = table(shifts, ends).T
    taps = table(shifts, np.ones(half))
    back = table(places[reach : reach + span], ends)
    halo = np.stack([left, right])
    return [t.astype(np.float32).astype(jnp.bfloat16) for t in (core, halo, lags, taps, back)] + [
        fixes.astype(np.float32)
    ]


def dot(left, right, left_dim=1, right_dim=0):
    return lax.dot_general(
        left,
        right,
        (((left_dim,), (right_dim,)), ((), ())),
        preferred_element_type=jnp.float32,
    )


def spectral_product(terms, sign):
    both = sum(p1 * q1 for (_, p1), (_, q1) in terms)
    real = sum(p0 * q0 for (p0, _), (q0, _) in terms)
    imag = sum(p1 * q0 - sign * (p0 * q1) for (p0, p1), (q0, q1) in terms)
    ends = lax.broadcasted_iota(jnp.int32, both.shape, 1) == 0
    return real + jnp.where(ends, 0.0, sign * both), jnp.where(ends, both, imag)


def fused_kernel(
    sizes, x_hbm, pairs_hbm, observed_hbm, mask_hbm, core_hbm, halo_hbm, lags_hbm, taps_hbm, back_hbm, fixes_hbm,
    out, pairs, core, halo, rest, observed, mask, core_table, halo_table, lags, taps, back, fixes,
    stage_sum, sum_across, stage_low, sum_low, sum_high, held_spec, core_spec, both_spec, first_core, first_left,
    full_spec, select, cross, stage_core, inbox_core, stage3, inbox3, inbox4, grads, stage6,
    high, load_sem, send1, recv1, send_sum, recv_sum, recv_high, core_send, core_recv, relay_send, relay_recv,
    send3, recv3, send4, recv4, send6, recv6,
):
    fibres, segs, recs = sizes
    bands = fibres * segs
    last = fibres - 1
    g, f, s, r = (lax.axis_index(name) for name in ("groups", "fibre", "seg", "rec"))
    o = 1 - s
    band = f * segs + s
    span, reach, width = S // bands, LAGS // 2, x_hbm.shape[1]
    n = span + LAGS
    half = n // 2
    blocks = width // BLOCK
    count = pairs.shape[1] * BLOCK
    own_count = count // recs
    low, full = jnp.bfloat16, jnp.float32

    def at(fibre, seg, rec):
        return (g, fibre, seg, rec)

    def at_band(index):
        return at(index // segs, index % segs, r)

    def remote(src, dst, send, recv, device):
        return pltpu.make_async_remote_copy(
            src_ref=src, dst_ref=dst, send_sem=send, recv_sem=recv,
            device_id=device, device_id_type=pl.DeviceIdType.MESH,
        )

    def push(src, dst, send, recv, device):
        copy = remote(src, dst, send, recv, device)
        copy.start()
        return copy

    def arrived(dst, recv):
        remote(dst, dst, recv, recv, at(f, s, 1 - r)).wait_recv()

    def signal(sem, device):
        pl.semaphore_signal(sem, inc=1, device_id=device, device_id_type=pl.DeviceIdType.MESH)

    def rows(start, size, unit):
        return pl.ds(pl.multiple_of(start, unit), size)

    def flipped(index, bits):
        result, bit = 0, 1
        while bit < bands:
            digit = index // bit % 2
            result += bit * (1 - digit if bits // bit % 2 else digit)
            bit *= 2
        return result

    partner = at(f, s, 1 - r)
    across = at(f, o, r)
    places = [(fi, si) for fi in range(fibres) for si in range(segs)]

    barrier = pltpu.get_barrier_semaphore()
    signal(barrier, partner)
    signal(barrier, across)
    for fi, si in places:

        @pl.when((fi >= f - 1) & (fi != f))
        def _():
            signal(barrier, at(fi, si, r))

    locals_ = [
        pltpu.make_async_copy(x_hbm.at[rows(span * s, span, reach)], core.at[s], load_sem.at[0]),
        pltpu.make_async_copy(x_hbm.at[rows(reach + reach * o, reach, reach)], halo.at[o, s], load_sem.at[1]),
        pltpu.make_async_copy(x_hbm.at[rows((2 * span - reach) * o, reach, reach)], rest, load_sem.at[2]),
    ]
    loads = [
        pltpu.make_async_copy(src, dst, load_sem.at[3 + i])
        for i, (src, dst) in enumerate(
            [
                (pairs_hbm, pairs), (core_hbm, core_table), (halo_hbm, halo_table), (fixes_hbm, fixes),
                (lags_hbm, lags), (observed_hbm.at[r], observed), (mask_hbm, mask), (taps_hbm, taps), (back_hbm, back),
            ]
        )
    ]
    for load in locals_ + loads:
        load.start()
    pl.semaphore_wait(barrier, segs * jnp.minimum(f + 2, fibres))
    after = push(
        x_hbm.at[pl.ds(2 * span - reach, reach)], halo.at[0, s], send1.at[0], recv1.at[2 + s],
        at((f + 1) % fibres, 0, r),
    )
    before = remote(
        x_hbm.at[pl.ds(0, reach)], halo.at[1, s], send1.at[1], recv1.at[4 + s], at((f + last) % fibres, 1, r)
    )
    core_cut = span // 2
    core_sends = [
        remote(
            x_hbm.at[rows(span * o + core_cut * i, core_cut, core_cut)], core.at[s, pl.ds(core_cut * i, core_cut)],
            send1.at[2 + i], recv1.at[6 + i], across,
        )
        for i in range(2)
    ]
    row = remote(
        x_hbm.at[rows(reach + reach * s, reach, reach)], halo.at[s, s], send1.at[4], recv1.at[1], across
    )

    @pl.when(s == 0)
    def _():
        core_sends[0].start()

    for fi, si in places:

        @pl.when(fi < f - 1)
        def _():
            signal(high, at(fi, si, r))

    for load in locals_:
        load.wait()
    folded = sum(
        part.astype(full).reshape(-1, 8, width).sum(axis=0) for part in (core[s], halo[o, s], rest[...])
    )
    odd = lax.broadcasted_iota(jnp.int32, folded.shape, 0) % 2 == 1
    sums = jnp.concatenate(
        [
            jnp.sum(folded, axis=0, keepdims=True),
            jnp.sum(jnp.where(odd, -folded, folded), axis=0, keepdims=True),
        ],
        axis=0,
    )
    stage_sum[...] = sums
    sends = [after, before, row] + core_sends
    sends.append(push(stage_sum, sum_across, send_sum.at[bands], recv_sum.at[0], across))
    sum_sends = [
        remote(stage_sum, sum_high.at[band], send_sum.at[fi * segs + si], recv_high.at[band], at(fi, si, r))
        for fi, si in places
    ]
    for (fi, si), copy in zip(places, sum_sends):

        @pl.when(fi < f)
        def _():
            copy.start()

    @pl.when(s == 1)
    def _():
        core_sends[0].start()

    core_sends[1].start()
    row.start()

    @pl.when(f > 0)
    def _():
        before.start()

    loads[0].wait()
    lane = lax.broadcasted_iota(jnp.int32, (1, 2 * own_count), 1)
    line = lax.broadcasted_iota(jnp.int32, select.shape[1:], 0)
    for h in range(recs):
        target = lane
        for side in range(2):
            for j in range(bands):
                first = side * own_count + j * BLOCK
                inside = (lane >= first) & (lane < first + BLOCK)
                target = jnp.where(inside, lane + (pairs[side, j * recs + h] * BLOCK - first), target)
        select[h] = jnp.where(line == target, 1.0, 0.0).astype(low)

    def put(spec, seg, value):
        spec[rows(seg * blocks, blocks, blocks)] = value.astype(low).reshape(blocks, BLOCK, n)

    def core_part(seg):
        part = dot(core[seg], core_table[...], 0, 0)
        held_spec[seg] = part
        put(core_spec, seg, part)

    loads[1].wait()
    core_part(s)
    arrived(sum_across, recv_sum.at[0])

    @pl.when(f > 0)
    def _():
        arrived(sum_low, recv_sum.at[1])

    stage_low[s] = stage_sum[...] + jnp.where(f > 0, sum_low[s], 0.0)
    stage_low[o] = sum_across[...] + jnp.where(f > 0, sum_low[o], 0.0)
    low_send = remote(stage_low, sum_low, send_sum.at[bands + 1], recv_sum.at[1], at((f + 1) % fibres, s, r))

    @pl.when(f < last)
    def _():
        low_send.start()

    for i in range(2):
        arrived(core.at[o, pl.ds(core_cut * i, core_cut)], recv1.at[6 + i])
    core_part(o)
    for fi, si in places:

        @pl.when(fi > f)
        def _():
            arrived(sum_high.at[fi * segs + si], recv_high.at[fi * segs + si])

    loads[2].wait()
    loads[3].wait()

    columns = []
    for seg in range(segs):
        total = stage_low[seg]
        for fi in range(1, fibres):
            total += jnp.where(fi > f, sum_high[fi * segs + seg], 0.0)
        columns.append(jnp.concatenate([total] * 4, axis=0).T)

    def fixed(value, seg, part):
        column = columns[seg]
        line = fixes[2 * part : 2 * part + 2, :]
        return value + (column[:, 0:1] * line[0:1] + column[:, 1:2] * line[1:2])

    for seg in range(segs):
        put(first_core, seg, fixed(held_spec[seg], seg, 0))

    @pl.when(s == 0)
    def _():
        for seg in range(segs):
            arrived(halo.at[0, seg], recv1.at[2 + seg])

    @pl.when(s == 1)
    def _():
        arrived(halo.at[0, 0], recv1.at[1])

    for seg in range(segs):
        part = dot(halo[0, seg], halo_table[0], 0, 0)
        put(first_left, seg, fixed(part, seg, 1))
        part += held_spec[seg]
        held_spec[seg] = part
        put(both_spec, seg, part)

    def block(spec, index):
        value = spec[index].astype(full)
        return value[:, :half], value[:, half:]

    cut = bands // 2

    def correlate(place, h, side):
        for i in range(cut):
            pair = (side * cut + i) * recs + h
            one, two = pairs[0, pair], pairs[1, pair]
            terms = [(block(first_core, one), block(both_spec, two)), (block(first_left, one), block(core_spec, two))]
            real, imag = spectral_product(terms, 1.0)
            here = pl.ds(i * BLOCK, BLOCK)
            cross[place, here, pl.ds(0, half)] = real.astype(low)
            cross[place, here, pl.ds(half, half)] = imag.astype(low)
        return dot(cross[place], lags[...])

    loads[4].wait()
    near = band // cut
    sides = (1 - near, near)
    for i, side in enumerate(sides):
        stage_core[i] = correlate(i, 1 - r, side).astype(low)
        sends.append(push(stage_core.at[i], inbox_core.at[i], core_send.at[i], core_recv.at[i], partner))

    @pl.when(f < last - 1)
    def _():
        pl.semaphore_wait(high, segs * (last - 1 - f))

    @pl.when(f == 0)
    def _():
        before.start()

    for i, side in enumerate(sides):
        partial = correlate(2 + i, r, side)
        arrived(inbox_core.at[i], core_recv.at[i])
        partial = (partial + inbox_core[i].astype(full)).astype(low)
        stage3[rows(side * cut, cut, cut)] = partial.reshape(cut, BLOCK, LAGS)
        for d in range(bands - 1 - i * cut, max(bands - 1 - (i + 1) * cut, 0), -1):
            j = flipped(band, d)
            sends.append(push(stage3.at[j], inbox3.at[band], send3.at[d - 1], recv3.at[band], at_band(j)))
    inbox3[band] = stage3[band]

    @pl.when(s == 0)
    def _():
        arrived(halo.at[1, 1], recv1.at[1])

    @pl.when(s == 1)
    def _():
        for seg in range(segs):
            arrived(halo.at[1, seg], recv1.at[4 + seg])

    for seg in range(segs):
        put(full_spec, seg, fixed(held_spec[seg] + dot(halo[1, seg], halo_table[1], 0, 0), seg, 2))
    loads[5].wait()
    loads[6].wait()
    for d in range(1, bands):
        k = flipped(band, d)
        arrived(inbox3.at[k], recv3.at[k])
    synthetic = inbox3[0].astype(full)
    for k in range(1, bands):
        synthetic += inbox3[k].astype(full)
    window = mask[pl.ds(r, 1), :].astype(full)
    inbox4[r, band] = (window * jnp.tanh(synthetic - observed[...])).astype(low)
    own = inbox4.at[r, band]
    for d in range(bands - 1, 0, -1):
        j = flipped(band, d)
        sends.append(push(own, own, send4.at[d - 1], recv4.at[band], at_band(j)))
    sends.append(push(own, own, relay_send.at[0], relay_recv.at[band], partner))
    for d in range(1, bands):
        k = flipped(band, d)
        arrived(inbox4.at[r, k], recv4.at[k])
        got = inbox4.at[r, k]
        sends.append(push(got, got, relay_send.at[d], relay_recv.at[k], partner))
    loads[7].wait()

    def gradients(h):
        spread = dot(inbox4[h].reshape(own_count, LAGS), taps[...])
        for j in range(bands):
            pair = j * recs + h
            filters = spread[j * BLOCK : (j + 1) * BLOCK]
            filters = filters[:, :half], filters[:, half:]
            first = block(full_spec, pairs[0, pair])
            second = block(full_spec, pairs[1, pair])
            for base, parts in (
                (j * BLOCK, spectral_product([(filters, second)], -1.0)),
                (own_count + j * BLOCK, spectral_product([(first, filters)], 1.0)),
            ):
                for p in range(2):
                    grads[pl.ds(base, BLOCK), pl.ds(p * half, half)] = parts[p].astype(low)

    def gathered(h, seg):
        return dot(select[h, rows(seg * width, width, width), :], grads[...])

    gradients(r)
    for seg in range(segs):
        held_spec[seg] = gathered(r, seg)
    for d in range(bands):
        k = flipped(band, d)
        arrived(inbox4.at[1 - r, k], relay_recv.at[k])
    gradients(1 - r)
    loads[8].wait()
    here = rows(span * s, span, span)
    there = rows(span * o, span, span)
    summed = (held_spec[o] + gathered(1 - r, o)).astype(low)
    for i in range(2):
        piece = pl.ds(i * core_cut, core_cut)
        stage6[piece, :] = dot(back[piece, :], summed, 1, 1).astype(low)
        dst = out.at[rows(span * s + i * core_cut, core_cut, core_cut), :]
        sends.append(push(stage6.at[piece], dst, send6.at[i], recv6.at[i], across))
    summed = (held_spec[s] + gathered(1 - r, s)).astype(low)
    out[here, :] = dot(back[...], summed, 1, 1).astype(low)
    for i in range(2):
        arrived(out.at[rows(span * o + i * core_cut, core_cut, core_cut), :], recv6.at[i])
    for copy in sends:
        copy.wait_send()
    for (fi, si), copy in zip(places, sum_sends):

        @pl.when(fi < f)
        def _():
            copy.wait_send()

    @pl.when(f < last)
    def _():
        low_send.wait_send()


def fused_on_device(mesh_shape, tables, records, pairs, observed, lag_mask):
    fibres, segs, recs = (mesh_shape[name] for name in ("fibre", "seg", "rec"))
    bands = fibres * segs
    _, extent, width = records.shape
    span, reach = S // bands, LAGS // 2
    n = span + LAGS
    count = pairs.shape[0] * BLOCK
    own = count // recs
    total = segs * width
    low, full = jnp.bfloat16, jnp.float32
    vmem = pl.BlockSpec(memory_space=pltpu.VMEM)
    hbm = pl.BlockSpec(memory_space=pltpu.HBM)
    corr = (BLOCK, LAGS)
    spec = pltpu.VMEM((total // BLOCK, BLOCK, n), low)

    def sems(*sizes):
        return [pltpu.SemaphoreType.DMA((size,)) for size in sizes]

    result = pl.pallas_call(
        functools.partial(fused_kernel, (fibres, segs, recs)),
        out_shape=pltpu.VMEM((extent, width), low),
        in_specs=[hbm] * 10,
        out_specs=vmem,
        scratch_shapes=[
            pltpu.SMEM((2, pairs.shape[0]), jnp.int32),
            pltpu.VMEM((segs, span, width), low),
            pltpu.VMEM((2, segs, reach, width), low),
            pltpu.VMEM((reach, width), low),
            pltpu.VMEM(corr, full),
            pltpu.VMEM(lag_mask.shape, jnp.int32),
            pltpu.VMEM((span, n), low),
            pltpu.VMEM((2, reach, n), low),
            pltpu.VMEM((n, LAGS), low),
            pltpu.VMEM((LAGS, n), low),
            pltpu.VMEM((span, n), low),
            pltpu.VMEM((8, n), full),
            pltpu.VMEM((2, width), full),
            pltpu.VMEM((2, width), full),
            pltpu.VMEM((segs, 2, width), full),
            pltpu.VMEM((segs, 2, width), full),
            pltpu.VMEM((bands, 2, width), full),
            pltpu.VMEM((segs, width, n), full),
            spec, spec, spec, spec, spec,
            pltpu.VMEM((recs, total, 2 * own), low),
            pltpu.VMEM((2 * recs, own // 2, n), low),
            pltpu.VMEM((2, own // 2, LAGS), low),
            pltpu.VMEM((2, own // 2, LAGS), low),
            pltpu.VMEM((bands,) + corr, low),
            pltpu.VMEM((bands,) + corr, low),
            pltpu.VMEM((recs, bands) + corr, low),
            pltpu.VMEM((2 * own, n), low),
            pltpu.VMEM((span, width), low),
            pltpu.SemaphoreType.REGULAR,
            *sems(12, 5, 8, bands + 2, 2, bands, 2, 2, bands, bands),
            *sems(bands - 1, bands, bands - 1, bands, 2, 2),
        ],
        compiler_params=pltpu.CompilerParams(
            has_side_effects=True, collective_id=0, vmem_limit_bytes=VMEM_GRANT
        ),
        name="adjoint",
    )(records[0], pairs.T, observed, lag_mask, *tables)
    return result[None]


def fits_fused(shape, records, pairs):
    fibres, segs, recs = (shape[name] for name in ("fibre", "seg", "rec"))
    bands = fibres * segs
    width = records.shape[2] // (shape["groups"] * segs)
    return (
        fibres > 1
        and fibres & (fibres - 1) == 0
        and segs == 2
        and recs == 2
        and width % 128 == 0
        and width * segs <= 512
        and S // bands >= LAGS
        and pairs.shape[0] == bands * recs
    )


def solution(mesh):
    in_specs = (
        P("rec", "fibre", ("groups", "seg")),
        P(),
        P(("groups", "fibre", "seg"), None, None),
        P(("groups", "fibre", "seg"), None),
    )
    out_specs = P("rec", "fibre", ("groups", "seg"))
    shape = dict(mesh.shape)

    def run(records, pairs, observed, lag_mask):
        args = (records, pairs, observed, lag_mask)
        if not fits_fused(shape, records, pairs):
            return jax.shard_map(
                on_device, mesh=mesh, in_specs=in_specs, out_specs=out_specs, check_vma=False
            )(*args)
        tables = [jnp.asarray(t) for t in window_tables(shape["fibre"] * shape["seg"])]

        def body(*blocks):
            return fused_on_device(shape, tables, *blocks)

        return jax.shard_map(
            body, mesh=mesh, in_specs=in_specs, out_specs=out_specs, check_vma=False
        )(*args)

    return run
```

time: 34.3 us -> 37.2 us (1.085)
  Pallas kernels: 33.4 us -> 36.3 us
    pallas_call x1, Pallas kernels: 33.4 us -> 36.3 us  [fused_on_device(): pl.pallas_call(functools.partial(fused_kernel, (fibres, segs, recs)), out...]
where the time goes in v2:
time: 37.2 us; the launch traced here: 37 us
  Pallas kernels  36.3 us (98%)
  local copies, waits for them, and re-layouts  0.71 us (2%)
    pallas_call x1, Pallas kernels, fused_on_device(): pl.pallas_call(functools.partial(fused_kernel, (fibres, segs, recs)), out...  36.3 us

profile of v2, /device:TPU:0, one launch (start us, length us, event | category | flops | bytes accessed | tf_op | source)
XLA Modules:
  0.0 37.0 jit_solution(10072952886922736425)
XLA Ops:
  0.0 36.3 %adjoint.1 = bf16[512,256]{1,0:T(8,128)(2,1)S(1)} custom-call(bf16[512,256]{1,0:T(8,128)(2,1)} %bitcast.4, s32[2,16]{1,0:T(2,128)} %bitcast.5, f32[2,32,256]{2,1,0:T(8,128)} %observed_hbm.1, s32[2,256]{1,0:T(2,128)} %mask_hbm.1, bf16[256,512]{1,0:T(8,128)(2,1)} %constant.12.clone.core_hbm, bf16[2,128,512]{2,1,0:T(8,128)(2,1)} %constant.13.clone.halo_hbm, ...), custom_call_target="tpu_custom_call" | custom-call | tf_op jit(solution)/shard_map/adjoint/pallas_call | solution.py:557
  36.3 0.7 %copy.12 = bf16[1,512,256]{2,1,0:T(8,128)(2,1)} copy(bf16[1,512,256]{2,1,0:T(8,128)(2,1)S(1)} %bitcast.3) | data formatting | bytes 524288

commit v3 on v2

--- a/solution.py
+++ b/solution.py
@@ -13,6 +13,7 @@
 LAGS = 256
 BLOCK = 32
 CH_DEV = 64
+PIECE = 32
 VMEM_GRANT = 60899328
 
 
@@ -150,16 +151,11 @@
 
     whole = table(places, np.ones(half))
     left, core, right = whole[:reach], whole[reach : reach + span], whole[reach + span :]
-    signs = np.where(places % 2 == 0, 1.0, -1.0)[:, None]
-    parts = (slice(reach, reach + span), slice(0, reach), slice(0, n), slice(0, 0))
-    fixes = np.stack([row for p in parts for row in (whole[p].sum(0), -(signs * whole)[p].sum(0))]) / S
     lags = table(shifts, ends).T
     taps = table(shifts, np.ones(half))
     back = table(places[reach : reach + span], ends)
     halo = np.stack([left, right])
-    return [t.astype(np.float32).astype(jnp.bfloat16) for t in (core, halo, lags, taps, back)] + [
-        fixes.astype(np.float32)
-    ]
+    return [t.astype(np.float32).astype(jnp.bfloat16) for t in (core, halo, lags, taps, back)]
 
 
 def dot(left, right, left_dim=1, right_dim=0):
@@ -180,11 +176,11 @@
 
 
 def fused_kernel(
-    sizes, x_hbm, pairs_hbm, observed_hbm, mask_hbm, core_hbm, halo_hbm, lags_hbm, taps_hbm, back_hbm, fixes_hbm,
-    out, pairs, core, halo, rest, observed, mask, core_table, halo_table, lags, taps, back, fixes,
-    stage_sum, sum_across, stage_low, sum_low, sum_high, held_spec, core_spec, both_spec, first_core, first_left,
+    sizes, x_hbm, pairs_hbm, observed_hbm, mask_hbm, core_hbm, halo_hbm, lags_hbm, taps_hbm, back_hbm,
+    out, pairs, core, halo, rest, observed, mask, core_table, halo_table, lags, taps, back,
+    inbox_sum, stage_total, inbox_total, columns, held_spec, core_spec, both_spec, left_spec,
     full_spec, select, cross, stage_core, inbox_core, stage3, inbox3, inbox4, grads, stage6,
-    high, load_sem, send1, recv1, send_sum, recv_sum, recv_high, core_send, core_recv, relay_send, relay_recv,
+    high, load_sem, send1, recv1, send_sum, recv_sum, total_sem, core_send, core_recv, relay_send, relay_recv,
     send3, recv3, send4, recv4, send6, recv6,
 ):
     fibres, segs, recs = sizes
@@ -235,6 +231,21 @@
             bit *= 2
         return result
 
+    class bulk:
+        def __init__(self, first, size, dst, send, recv, device):
+            self.whole = remote(x_hbm.at[rows(first, size, PIECE)], dst, send, recv, device)
+            self.pieces = [
+                remote(x_hbm.at[rows(first + i, PIECE, PIECE)], dst.at[pl.ds(i, PIECE)], send, recv, device)
+                for i in range(0, size, PIECE)
+            ]
+
+        def start(self):
+            for piece in self.pieces:
+                piece.start()
+
+        def wait_send(self):
+            self.whole.wait_send()
+
     partner = at(f, s, 1 - r)
     across = at(f, o, r)
     places = [(fi, si) for fi in range(fibres) for si in range(segs)]
@@ -257,36 +268,34 @@
         pltpu.make_async_copy(src, dst, load_sem.at[3 + i])
         for i, (src, dst) in enumerate(
             [
-                (pairs_hbm, pairs), (core_hbm, core_table), (halo_hbm, halo_table), (fixes_hbm, fixes),
-                (lags_hbm, lags), (observed_hbm.at[r], observed), (mask_hbm, mask), (taps_hbm, taps), (back_hbm, back),
+                (pairs_hbm, pairs), (core_hbm, core_table), (halo_hbm, halo_table), (lags_hbm, lags), (observed_hbm.at[r], observed), (mask_hbm, mask), (taps_hbm, taps), (back_hbm, back),
             ]
         )
     ]
     for load in locals_ + loads:
         load.start()
     pl.semaphore_wait(barrier, segs * jnp.minimum(f + 2, fibres))
-    after = push(
-        x_hbm.at[pl.ds(2 * span - reach, reach)], halo.at[0, s], send1.at[0], recv1.at[2 + s],
-        at((f + 1) % fibres, 0, r),
-    )
-    before = remote(
-        x_hbm.at[pl.ds(0, reach)], halo.at[1, s], send1.at[1], recv1.at[4 + s], at((f + last) % fibres, 1, r)
-    )
+    after = bulk(
+        2 * span - reach, reach, halo.at[0, s], send1.at[0], recv1.at[2 + s], at((f + 1) % fibres, 0, r)
+    )
+    before = bulk(0, reach, halo.at[1, s], send1.at[1], recv1.at[4 + s], at((f + last) % fibres, 1, r))
     core_cut = span // 2
-    core_sends = [
-        remote(
-            x_hbm.at[rows(span * o + core_cut * i, core_cut, core_cut)], core.at[s, pl.ds(core_cut * i, core_cut)],
-            send1.at[2 + i], recv1.at[6 + i], across,
-        )
-        for i in range(2)
-    ]
-    row = remote(
-        x_hbm.at[rows(reach + reach * s, reach, reach)], halo.at[s, s], send1.at[4], recv1.at[1], across
-    )
+    core_sends = bulk(span * o, span, core.at[s], send1.at[2], recv1.at[0], across)
+    row = bulk(reach + reach * s, reach, halo.at[s, s], send1.at[4], recv1.at[1], across)
+
+    @pl.when((f < last))
+    def _():
+        after.start()
+
+    core_sends.start()
 
     @pl.when(s == 0)
     def _():
-        core_sends[0].start()
+        row.start()
+
+    @pl.when(f == last)
+    def _():
+        after.start()
 
     for fi, si in places:
 
@@ -300,36 +309,25 @@
         part.astype(full).reshape(-1, 8, width).sum(axis=0) for part in (core[s], halo[o, s], rest[...])
     )
     odd = lax.broadcasted_iota(jnp.int32, folded.shape, 0) % 2 == 1
-    sums = jnp.concatenate(
+    inbox_sum[band] = jnp.concatenate(
         [
             jnp.sum(folded, axis=0, keepdims=True),
             jnp.sum(jnp.where(odd, -folded, folded), axis=0, keepdims=True),
         ],
         axis=0,
     )
-    stage_sum[...] = sums
-    sends = [after, before, row] + core_sends
-    sends.append(push(stage_sum, sum_across, send_sum.at[bands], recv_sum.at[0], across))
+    sends = [after, before, row, core_sends]
+    own_sum = inbox_sum.at[band]
     sum_sends = [
-        remote(stage_sum, sum_high.at[band], send_sum.at[fi * segs + si], recv_high.at[band], at(fi, si, r))
-        for fi, si in places
+        remote(own_sum, own_sum, send_sum.at[fi * segs + si], recv_sum.at[band], at(fi, si, r)) for fi, si in places
     ]
+    across_sum = push(own_sum, own_sum, send_sum.at[bands], recv_sum.at[band], across)
+    sends.append(across_sum)
     for (fi, si), copy in zip(places, sum_sends):
 
         @pl.when(fi < f)
         def _():
             copy.start()
-
-    @pl.when(s == 1)
-    def _():
-        core_sends[0].start()
-
-    core_sends[1].start()
-    row.start()
-
-    @pl.when(f > 0)
-    def _():
-        before.start()
 
     loads[0].wait()
     lane = lax.broadcasted_iota(jnp.int32, (1, 2 * own_count), 1)
@@ -353,46 +351,9 @@
 
     loads[1].wait()
     core_part(s)
-    arrived(sum_across, recv_sum.at[0])
-
-    @pl.when(f > 0)
-    def _():
-        arrived(sum_low, recv_sum.at[1])
-
-    stage_low[s] = stage_sum[...] + jnp.where(f > 0, sum_low[s], 0.0)
-    stage_low[o] = sum_across[...] + jnp.where(f > 0, sum_low[o], 0.0)
-    low_send = remote(stage_low, sum_low, send_sum.at[bands + 1], recv_sum.at[1], at((f + 1) % fibres, s, r))
-
-    @pl.when(f < last)
-    def _():
-        low_send.start()
-
-    for i in range(2):
-        arrived(core.at[o, pl.ds(core_cut * i, core_cut)], recv1.at[6 + i])
+    arrived(core.at[o], recv1.at[0])
     core_part(o)
-    for fi, si in places:
-
-        @pl.when(fi > f)
-        def _():
-            arrived(sum_high.at[fi * segs + si], recv_high.at[fi * segs + si])
-
     loads[2].wait()
-    loads[3].wait()
-
-    columns = []
-    for seg in range(segs):
-        total = stage_low[seg]
-        for fi in range(1, fibres):
-            total += jnp.where(fi > f, sum_high[fi * segs + seg], 0.0)
-        columns.append(jnp.concatenate([total] * 4, axis=0).T)
-
-    def fixed(value, seg, part):
-        column = columns[seg]
-        line = fixes[2 * part : 2 * part + 2, :]
-        return value + (column[:, 0:1] * line[0:1] + column[:, 1:2] * line[1:2])
-
-    for seg in range(segs):
-        put(first_core, seg, fixed(held_spec[seg], seg, 0))
 
     @pl.when(s == 0)
     def _():
@@ -405,7 +366,7 @@
 
     for seg in range(segs):
         part = dot(halo[0, seg], halo_table[0], 0, 0)
-        put(first_left, seg, fixed(part, seg, 1))
+        put(left_spec, seg, part)
         part += held_spec[seg]
         held_spec[seg] = part
         put(both_spec, seg, part)
@@ -420,14 +381,14 @@
         for i in range(cut):
             pair = (side * cut + i) * recs + h
             one, two = pairs[0, pair], pairs[1, pair]
-            terms = [(block(first_core, one), block(both_spec, two)), (block(first_left, one), block(core_spec, two))]
+            terms = [(block(core_spec, one), block(both_spec, two)), (block(left_spec, one), block(core_spec, two))]
             real, imag = spectral_product(terms, 1.0)
             here = pl.ds(i * BLOCK, BLOCK)
             cross[place, here, pl.ds(0, half)] = real.astype(low)
             cross[place, here, pl.ds(half, half)] = imag.astype(low)
         return dot(cross[place], lags[...])
 
-    loads[4].wait()
+    loads[3].wait()
     near = band // cut
     sides = (1 - near, near)
     for i, side in enumerate(sides):
@@ -438,9 +399,11 @@
     def _():
         pl.semaphore_wait(high, segs * (last - 1 - f))
 
-    @pl.when(f == 0)
-    def _():
-        before.start()
+    for (fi, si), copy in zip(places, sum_sends):
+
+        @pl.when(fi > f)
+        def _():
+            copy.start()
 
     for i, side in enumerate(sides):
         partial = correlate(2 + i, r, side)
@@ -452,6 +415,12 @@
             sends.append(push(stage3.at[j], inbox3.at[band], send3.at[d - 1], recv3.at[band], at_band(j)))
     inbox3[band] = stage3[band]
 
+    @pl.when(s == 1)
+    def _():
+        row.start()
+
+    before.start()
+
     @pl.when(s == 0)
     def _():
         arrived(halo.at[1, 1], recv1.at[1])
@@ -461,14 +430,39 @@
         for seg in range(segs):
             arrived(halo.at[1, seg], recv1.at[4 + seg])
 
+    for d in range(1, bands):
+        k = flipped(band, d)
+        arrived(inbox_sum.at[k], recv_sum.at[k])
     for seg in range(segs):
-        put(full_spec, seg, fixed(held_spec[seg] + dot(halo[1, seg], halo_table[1], 0, 0), seg, 2))
+        stage_total[seg] = sum(inbox_sum[fi * segs + seg] for fi in range(fibres))
+    sends.append(push(stage_total, inbox_total, total_sem.at[0], total_sem.at[1], partner))
+    head = lax.broadcasted_iota(jnp.int32, (1, half), 1) == 0
+    for seg in range(segs):
+        total = jnp.concatenate([stage_total[seg]] * 4, axis=0).T * (n / S)
+        value = held_spec[seg] + dot(halo[1, seg], halo_table[1], 0, 0)
+        value = jnp.concatenate(
+            [
+                value[:, :half] + jnp.where(head, total[:, 0:1], 0.0),
+                value[:, half:] - jnp.where(head, total[:, 1:2], 0.0),
+            ],
+            axis=1,
+        )
+        put(full_spec, seg, value)
+    arrived(inbox_total, total_sem.at[1])
+    for seg in range(segs):
+        total = jnp.concatenate([stage_total[seg], inbox_total[seg]] * 2, axis=0)
+        columns[pl.ds(seg * blocks, blocks)] = total.T.reshape(blocks, BLOCK, 8)
+    loads[4].wait()
     loads[5].wait()
-    loads[6].wait()
+    ends = columns[pairs[0, band * recs + r]] * columns[pairs[1, band * recs + r]]
+    flat = ends[:, 0:1] + ends[:, 2:3]
+    alternating = ends[:, 1:2] + ends[:, 3:4]
+    even = lax.broadcasted_iota(jnp.int32, (BLOCK, LAGS), 1) % 2 == reach % 2
+    offset = (flat + jnp.where(even, -alternating, alternating)) * (1.0 / (2.0 * S * F**0.5))
     for d in range(1, bands):
         k = flipped(band, d)
         arrived(inbox3.at[k], recv3.at[k])
-    synthetic = inbox3[0].astype(full)
+    synthetic = offset + inbox3[0].astype(full)
     for k in range(1, bands):
         synthetic += inbox3[k].astype(full)
     window = mask[pl.ds(r, 1), :].astype(full)
@@ -483,7 +477,7 @@
         arrived(inbox4.at[r, k], recv4.at[k])
         got = inbox4.at[r, k]
         sends.append(push(got, got, relay_send.at[d], relay_recv.at[k], partner))
-    loads[7].wait()
+    loads[6].wait()
 
     def gradients(h):
         spread = dot(inbox4[h].reshape(own_count, LAGS), taps[...])
@@ -510,7 +504,7 @@
         k = flipped(band, d)
         arrived(inbox4.at[1 - r, k], relay_recv.at[k])
     gradients(1 - r)
-    loads[8].wait()
+    loads[7].wait()
     here = rows(span * s, span, span)
     there = rows(span * o, span, span)
     summed = (held_spec[o] + gathered(1 - r, o)).astype(low)
@@ -527,13 +521,9 @@
         copy.wait_send()
     for (fi, si), copy in zip(places, sum_sends):
 
-        @pl.when(fi < f)
+        @pl.when(fi != f)
         def _():
             copy.wait_send()
-
-    @pl.when(f < last)
-    def _():
-        low_send.wait_send()
 
 
 def fused_on_device(mesh_shape, tables, records, pairs, observed, lag_mask):
@@ -557,7 +547,7 @@
     result = pl.pallas_call(
         functools.partial(fused_kernel, (fibres, segs, recs)),
         out_shape=pltpu.VMEM((extent, width), low),
-        in_specs=[hbm] * 10,
+        in_specs=[hbm] * 9,
         out_specs=vmem,
         scratch_shapes=[
             pltpu.SMEM((2, pairs.shape[0]), jnp.int32),
@@ -571,14 +561,12 @@
             pltpu.VMEM((n, LAGS), low),
             pltpu.VMEM((LAGS, n), low),
             pltpu.VMEM((span, n), low),
-            pltpu.VMEM((8, n), full),
-            pltpu.VMEM((2, width), full),
-            pltpu.VMEM((2, width), full),
+            pltpu.VMEM((bands, 2, width), full),
             pltpu.VMEM((segs, 2, width), full),
             pltpu.VMEM((segs, 2, width), full),
-            pltpu.VMEM((bands, 2, width), full),
+            pltpu.VMEM((total // BLOCK, BLOCK, 8), full),
             pltpu.VMEM((segs, width, n), full),
-            spec, spec, spec, spec, spec,
+            spec, spec, spec, spec,
             pltpu.VMEM((recs, total, 2 * own), low),
             pltpu.VMEM((2 * recs, own // 2, n), low),
             pltpu.VMEM((2, own // 2, LAGS), low),
@@ -589,7 +577,7 @@
             pltpu.VMEM((2 * own, n), low),
             pltpu.VMEM((span, width), low),
             pltpu.SemaphoreType.REGULAR,
-            *sems(12, 5, 8, bands + 2, 2, bands, 2, 2, bands, bands),
+            *sems(11, 5, 8, bands + 1, bands, 2, 2, 2, bands, bands),
             *sems(bands - 1, bands, bands - 1, bands, 2, 2),
         ],
         compiler_params=pltpu.CompilerParams(

time: 37.2 us -> 33.6 us (0.903)
  Pallas kernels: 36.3 us -> 32.7 us
    pallas_call x1, Pallas kernels: 36.3 us -> 32.7 us  [fused_on_device(): pl.pallas_call(functools.partial(fused_kernel, (fibres, segs, recs)), out...]
where the time goes in v3:
time: 33.6 us; the launch traced here: 33.4 us
  Pallas kernels  32.7 us (97%)
  local copies, waits for them, and re-layouts  0.71 us (2%)
    pallas_call x1, Pallas kernels, fused_on_device(): pl.pallas_call(functools.partial(fused_kernel, (fibres, segs, recs)), out...  32.7 us
    unnamed x1, local copies, waits for them, and re-layouts  0.71 us

profile of v3, /device:TPU:0, one launch (start us, length us, event | category | flops | bytes accessed | tf_op | source)
XLA Modules:
  0.0 33.4 jit_solution(13258887251424795706)
XLA Ops:
  0.0 32.7 %adjoint.1 = bf16[512,256]{1,0:T(8,128)(2,1)S(1)} custom-call(bf16[512,256]{1,0:T(8,128)(2,1)} %bitcast.4, s32[2,16]{1,0:T(2,128)} %bitcast.5, f32[2,32,256]{2,1,0:T(8,128)} %observed_hbm.1, s32[2,256]{1,0:T(2,128)} %mask_hbm.1, bf16[256,512]{1,0:T(8,128)(2,1)} %constant.10.clone.core_hbm, bf16[2,128,512]{2,1,0:T(8,128)(2,1)} %constant.11.clone.halo_hbm, ...), custom_call_target="tpu_custom_call" | custom-call | tf_op jit(solution)/shard_map/adjoint/pallas_call | solution.py:547
  32.7 0.7 %copy.11 = bf16[1,512,256]{2,1,0:T(8,128)(2,1)} copy(bf16[1,512,256]{2,1,0:T(8,128)(2,1)S(1)} %bitcast.3) | data formatting | bytes 524288

commit v4 on v3

--- a/solution.py
+++ b/solution.py
@@ -180,7 +180,7 @@
     out, pairs, core, halo, rest, observed, mask, core_table, halo_table, lags, taps, back,
     inbox_sum, stage_total, inbox_total, columns, held_spec, core_spec, both_spec, left_spec,
     full_spec, select, cross, stage_core, inbox_core, stage3, inbox3, inbox4, grads, stage6,
-    high, load_sem, send1, recv1, send_sum, recv_sum, total_sem, core_send, core_recv, relay_send, relay_recv,
+    following, high, load_sem, send1, recv1, send_sum, recv_sum, total_sem, core_send, core_recv, relay_send, relay_recv,
     send3, recv3, send4, recv4, send6, recv6,
 ):
     fibres, segs, recs = sizes
@@ -194,7 +194,6 @@
     half = n // 2
     blocks = width // BLOCK
     count = pairs.shape[1] * BLOCK
-    own_count = count // recs
     low, full = jnp.bfloat16, jnp.float32
 
     def at(fibre, seg, rec):
@@ -255,7 +254,7 @@
     signal(barrier, across)
     for fi, si in places:
 
-        @pl.when((fi >= f - 1) & (fi != f))
+        @pl.when(fi > f)
         def _():
             signal(barrier, at(fi, si, r))
 
@@ -274,7 +273,7 @@
     ]
     for load in locals_ + loads:
         load.start()
-    pl.semaphore_wait(barrier, segs * jnp.minimum(f + 2, fibres))
+    pl.semaphore_wait(barrier, segs * (f + 1))
     after = bulk(
         2 * span - reach, reach, halo.at[0, s], send1.at[0], recv1.at[2 + s], at((f + 1) % fibres, 0, r)
     )
@@ -283,21 +282,17 @@
     core_sends = bulk(span * o, span, core.at[s], send1.at[2], recv1.at[0], across)
     row = bulk(reach + reach * s, reach, halo.at[s, s], send1.at[4], recv1.at[1], across)
 
-    @pl.when((f < last))
-    def _():
-        after.start()
-
     core_sends.start()
 
     @pl.when(s == 0)
     def _():
         row.start()
 
-    @pl.when(f == last)
-    def _():
-        after.start()
-
     for fi, si in places:
+
+        @pl.when(fi == f - 1)
+        def _():
+            signal(following, at(fi, si, r))
 
         @pl.when(fi < f - 1)
         def _():
@@ -330,16 +325,20 @@
             copy.start()
 
     loads[0].wait()
-    lane = lax.broadcasted_iota(jnp.int32, (1, 2 * own_count), 1)
-    line = lax.broadcasted_iota(jnp.int32, select.shape[1:], 0)
-    for h in range(recs):
-        target = lane
-        for side in range(2):
-            for j in range(bands):
-                first = side * own_count + j * BLOCK
+    cut = bands // 2
+    near = band // cut
+    groups = [(r, near), (r, 1 - near), (1 - r, near), (1 - r, 1 - near)]
+    group = 2 * cut * BLOCK
+    lane = lax.broadcasted_iota(jnp.int32, (1, 2 * count), 1)
+    target = lane
+    for p, (h, side) in enumerate(groups):
+        for end in range(2):
+            for i in range(cut):
+                first = p * group + (end * cut + i) * BLOCK
                 inside = (lane >= first) & (lane < first + BLOCK)
-                target = jnp.where(inside, lane + (pairs[side, j * recs + h] * BLOCK - first), target)
-        select[h] = jnp.where(line == target, 1.0, 0.0).astype(low)
+                target = jnp.where(inside, lane + (pairs[end, (side * cut + i) * recs + h] * BLOCK - first), target)
+    line = lax.broadcasted_iota(jnp.int32, select.shape, 0)
+    select[...] = jnp.where(line == target, 1.0, 0.0).astype(low)
 
     def put(spec, seg, value):
         spec[rows(seg * blocks, blocks, blocks)] = value.astype(low).reshape(blocks, BLOCK, n)
@@ -351,31 +350,62 @@
 
     loads[1].wait()
     core_part(s)
+
+    @pl.when(f < last)
+    def _():
+        pl.semaphore_wait(following, segs)
+
+    after.start()
     arrived(core.at[o], recv1.at[0])
     core_part(o)
+
+    @pl.when(f < last - 1)
+    def _():
+        pl.semaphore_wait(high, segs * (last - 1 - f))
+
+    for (fi, si), copy in zip(places, sum_sends):
+
+        @pl.when(fi > f)
+        def _():
+            copy.start()
+
+    @pl.when(f == 0)
+    def _():
+        before.start()
+
     loads[2].wait()
 
-    @pl.when(s == 0)
-    def _():
-        for seg in range(segs):
-            arrived(halo.at[0, seg], recv1.at[2 + seg])
-
-    @pl.when(s == 1)
-    def _():
-        arrived(halo.at[0, 0], recv1.at[1])
-
-    for seg in range(segs):
+    def left_part(seg):
         part = dot(halo[0, seg], halo_table[0], 0, 0)
         put(left_spec, seg, part)
         part += held_spec[seg]
         held_spec[seg] = part
         put(both_spec, seg, part)
 
+    @pl.when(s == 0)
+    def _():
+        arrived(halo.at[0, 0], recv1.at[2])
+
+    left_part(s)
+
+    @pl.when(s == 0)
+    def _():
+        arrived(halo.at[0, 1], recv1.at[3])
+
+    @pl.when(s == 1)
+    def _():
+        arrived(halo.at[0, 0], recv1.at[1])
+        row.start()
+
+    @pl.when(f > 0)
+    def _():
+        before.start()
+
+    left_part(o)
+
     def block(spec, index):
         value = spec[index].astype(full)
         return value[:, :half], value[:, half:]
-
-    cut = bands // 2
 
     def correlate(place, h, side):
         for i in range(cut):
@@ -389,46 +419,27 @@
         return dot(cross[place], lags[...])
 
     loads[3].wait()
-    near = band // cut
-    sides = (1 - near, near)
+    sides = (1, 0)
     for i, side in enumerate(sides):
         stage_core[i] = correlate(i, 1 - r, side).astype(low)
         sends.append(push(stage_core.at[i], inbox_core.at[i], core_send.at[i], core_recv.at[i], partner))
 
-    @pl.when(f < last - 1)
-    def _():
-        pl.semaphore_wait(high, segs * (last - 1 - f))
-
-    for (fi, si), copy in zip(places, sum_sends):
-
-        @pl.when(fi > f)
-        def _():
-            copy.start()
-
+    spread3 = [
+        remote(stage3.at[j], inbox3.at[band], send3.at[j], recv3.at[band], at(j // segs, j % segs, r))
+        for j in range(bands)
+    ]
     for i, side in enumerate(sides):
         partial = correlate(2 + i, r, side)
         arrived(inbox_core.at[i], core_recv.at[i])
         partial = (partial + inbox_core[i].astype(full)).astype(low)
         stage3[rows(side * cut, cut, cut)] = partial.reshape(cut, BLOCK, LAGS)
-        for d in range(bands - 1 - i * cut, max(bands - 1 - (i + 1) * cut, 0), -1):
-            j = flipped(band, d)
-            sends.append(push(stage3.at[j], inbox3.at[band], send3.at[d - 1], recv3.at[band], at_band(j)))
+        for j in range((side + 1) * cut - 1, side * cut - 1, -1):
+
+            @pl.when(band != j)
+            def _():
+                spread3[j].start()
+
     inbox3[band] = stage3[band]
-
-    @pl.when(s == 1)
-    def _():
-        row.start()
-
-    before.start()
-
-    @pl.when(s == 0)
-    def _():
-        arrived(halo.at[1, 1], recv1.at[1])
-
-    @pl.when(s == 1)
-    def _():
-        for seg in range(segs):
-            arrived(halo.at[1, seg], recv1.at[4 + seg])
 
     for d in range(1, bands):
         k = flipped(band, d)
@@ -436,18 +447,6 @@
     for seg in range(segs):
         stage_total[seg] = sum(inbox_sum[fi * segs + seg] for fi in range(fibres))
     sends.append(push(stage_total, inbox_total, total_sem.at[0], total_sem.at[1], partner))
-    head = lax.broadcasted_iota(jnp.int32, (1, half), 1) == 0
-    for seg in range(segs):
-        total = jnp.concatenate([stage_total[seg]] * 4, axis=0).T * (n / S)
-        value = held_spec[seg] + dot(halo[1, seg], halo_table[1], 0, 0)
-        value = jnp.concatenate(
-            [
-                value[:, :half] + jnp.where(head, total[:, 0:1], 0.0),
-                value[:, half:] - jnp.where(head, total[:, 1:2], 0.0),
-            ],
-            axis=1,
-        )
-        put(full_spec, seg, value)
     arrived(inbox_total, total_sem.at[1])
     for seg in range(segs):
         total = jnp.concatenate([stage_total[seg], inbox_total[seg]] * 2, axis=0)
@@ -468,57 +467,86 @@
     window = mask[pl.ds(r, 1), :].astype(full)
     inbox4[r, band] = (window * jnp.tanh(synthetic - observed[...])).astype(low)
     own = inbox4.at[r, band]
-    for d in range(bands - 1, 0, -1):
-        j = flipped(band, d)
-        sends.append(push(own, own, send4.at[d - 1], recv4.at[band], at_band(j)))
+    spread4 = [
+        remote(own, own, send4.at[j], recv4.at[band], at(j // segs, j % segs, r)) for j in range(bands)
+    ]
+    for j in range(bands):
+
+        @pl.when(band != j)
+        def _():
+            spread4[j].start()
+
     sends.append(push(own, own, relay_send.at[0], relay_recv.at[band], partner))
+
+    @pl.when(s == 0)
+    def _():
+        arrived(halo.at[1, 1], recv1.at[1])
+
+    @pl.when(s == 1)
+    def _():
+        for seg in range(segs):
+            arrived(halo.at[1, seg], recv1.at[4 + seg])
+
+    head = lax.broadcasted_iota(jnp.int32, (1, half), 1) == 0
+    for seg in range(segs):
+        total = jnp.concatenate([stage_total[seg]] * 4, axis=0).T * (n / S)
+        value = held_spec[seg] + dot(halo[1, seg], halo_table[1], 0, 0)
+        value = jnp.concatenate(
+            [
+                value[:, :half] + jnp.where(head, total[:, 0:1], 0.0),
+                value[:, half:] - jnp.where(head, total[:, 1:2], 0.0),
+            ],
+            axis=1,
+        )
+        put(full_spec, seg, value)
+    loads[6].wait()
+
+    def gradients(p):
+        h, side = groups[p]
+        spread = dot(inbox4[h, pl.ds(side * cut, cut)].reshape(cut * BLOCK, LAGS), taps[...])
+        for i in range(cut):
+            pair = (side * cut + i) * recs + h
+            filters = spread[i * BLOCK : (i + 1) * BLOCK]
+            filters = filters[:, :half], filters[:, half:]
+            first = block(full_spec, pairs[0, pair])
+            second = block(full_spec, pairs[1, pair])
+            base = p * group + i * BLOCK
+            for start, parts in (
+                (base, spectral_product([(filters, second)], -1.0)),
+                (base + cut * BLOCK, spectral_product([(first, filters)], 1.0)),
+            ):
+                for q in range(2):
+                    grads[pl.ds(start, BLOCK), pl.ds(q * half, half)] = parts[q].astype(low)
+
     for d in range(1, bands):
         k = flipped(band, d)
         arrived(inbox4.at[r, k], recv4.at[k])
         got = inbox4.at[r, k]
         sends.append(push(got, got, relay_send.at[d], relay_recv.at[k], partner))
-    loads[6].wait()
-
-    def gradients(h):
-        spread = dot(inbox4[h].reshape(own_count, LAGS), taps[...])
-        for j in range(bands):
-            pair = j * recs + h
-            filters = spread[j * BLOCK : (j + 1) * BLOCK]
-            filters = filters[:, :half], filters[:, half:]
-            first = block(full_spec, pairs[0, pair])
-            second = block(full_spec, pairs[1, pair])
-            for base, parts in (
-                (j * BLOCK, spectral_product([(filters, second)], -1.0)),
-                (own_count + j * BLOCK, spectral_product([(first, filters)], 1.0)),
-            ):
-                for p in range(2):
-                    grads[pl.ds(base, BLOCK), pl.ds(p * half, half)] = parts[p].astype(low)
-
-    def gathered(h, seg):
-        return dot(select[h, rows(seg * width, width, width), :], grads[...])
-
-    gradients(r)
-    for seg in range(segs):
-        held_spec[seg] = gathered(r, seg)
-    for d in range(bands):
-        k = flipped(band, d)
-        arrived(inbox4.at[1 - r, k], relay_recv.at[k])
-    gradients(1 - r)
+    for p, (first, stop) in enumerate(((0, 0), (0, 0), (0, cut), (cut, bands))):
+        for d in range(first, stop):
+            k = flipped(band, d)
+            arrived(inbox4.at[1 - r, k], relay_recv.at[k])
+        gradients(p)
     loads[7].wait()
+
+    def summed(seg):
+        return dot(select[rows(seg * width, width, width), :], grads[...]).astype(low)
+
+    stage6[...] = dot(back[...], summed(o), 1, 1).astype(low)
     here = rows(span * s, span, span)
-    there = rows(span * o, span, span)
-    summed = (held_spec[o] + gathered(1 - r, o)).astype(low)
-    for i in range(2):
-        piece = pl.ds(i * core_cut, core_cut)
-        stage6[piece, :] = dot(back[piece, :], summed, 1, 1).astype(low)
-        dst = out.at[rows(span * s + i * core_cut, core_cut, core_cut), :]
-        sends.append(push(stage6.at[piece], dst, send6.at[i], recv6.at[i], across))
-    summed = (held_spec[s] + gathered(1 - r, s)).astype(low)
-    out[here, :] = dot(back[...], summed, 1, 1).astype(low)
-    for i in range(2):
-        arrived(out.at[rows(span * o + i * core_cut, core_cut, core_cut), :], recv6.at[i])
+    sends.append(push(stage6, out.at[here, :], send6.at[0], recv6.at[0], across))
+    out[here, :] = dot(back[...], summed(s), 1, 1).astype(low)
+    arrived(out.at[rows(span * o, span, span), :], recv6.at[0])
     for copy in sends:
         copy.wait_send()
+    for j in range(bands):
+
+        @pl.when(band != j)
+        def _():
+            spread3[j].wait_send()
+            spread4[j].wait_send()
+
     for (fi, si), copy in zip(places, sum_sends):
 
         @pl.when(fi != f)
@@ -567,18 +595,19 @@
             pltpu.VMEM((total // BLOCK, BLOCK, 8), full),
             pltpu.VMEM((segs, width, n), full),
             spec, spec, spec, spec,
-            pltpu.VMEM((recs, total, 2 * own), low),
+            pltpu.VMEM((total, 2 * count), low),
             pltpu.VMEM((2 * recs, own // 2, n), low),
             pltpu.VMEM((2, own // 2, LAGS), low),
             pltpu.VMEM((2, own // 2, LAGS), low),
             pltpu.VMEM((bands,) + corr, low),
             pltpu.VMEM((bands,) + corr, low),
             pltpu.VMEM((recs, bands) + corr, low),
-            pltpu.VMEM((2 * own, n), low),
+            pltpu.VMEM((2 * count, n), low),
             pltpu.VMEM((span, width), low),
             pltpu.SemaphoreType.REGULAR,
+            pltpu.SemaphoreType.REGULAR,
             *sems(11, 5, 8, bands + 1, bands, 2, 2, 2, bands, bands),
-            *sems(bands - 1, bands, bands - 1, bands, 2, 2),
+            *sems(bands, bands, bands, bands, 2, 2),
         ],
         compiler_params=pltpu.CompilerParams(
             has_side_effects=True, collective_id=0, vmem_limit_bytes=VMEM_GRANT

time: 33.6 us -> 30.4 us (0.905)
  Pallas kernels: 32.7 us -> 29.5 us
    pallas_call x1, Pallas kernels: 32.7 us -> 29.5 us  [fused_on_device(): pl.pallas_call(functools.partial(fused_kernel, (fibres, segs, recs)), out...]
where the time goes in v4:
time: 30.4 us; the launch traced here: 30.3 us
  Pallas kernels  29.5 us (97%)
  local copies, waits for them, and re-layouts  0.71 us (2%)
    pallas_call x1, Pallas kernels, fused_on_device(): pl.pallas_call(functools.partial(fused_kernel, (fibres, segs, recs)), out...  29.5 us
    unnamed x1, local copies, waits for them, and re-layouts  0.71 us

profile of v4, /device:TPU:0, one launch (start us, length us, event | category | flops | bytes accessed | tf_op | source)
XLA Modules:
  0.0 30.3 jit_solution(12193397194976600967)
XLA Ops:
  0.0 29.5 %adjoint.1 = bf16[512,256]{1,0:T(8,128)(2,1)S(1)} custom-call(bf16[512,256]{1,0:T(8,128)(2,1)} %bitcast.4, s32[2,16]{1,0:T(2,128)} %bitcast.5, f32[2,32,256]{2,1,0:T(8,128)} %observed_hbm.1, s32[2,256]{1,0:T(2,128)} %mask_hbm.1, bf16[256,512]{1,0:T(8,128)(2,1)} %constant.10.clone.core_hbm, bf16[2,128,512]{2,1,0:T(8,128)(2,1)} %constant.11.clone.halo_hbm, ...), custom_call_target="tpu_custom_call" | custom-call | tf_op jit(solution)/shard_map/adjoint/pallas_call | solution.py:575
  29.5 0.7 %copy.11 = bf16[1,512,256]{2,1,0:T(8,128)(2,1)} copy(bf16[1,512,256]{2,1,0:T(8,128)(2,1)S(1)} %bitcast.3) | data formatting | bytes 524288

commit v5 on v4

--- a/solution.py
+++ b/solution.py
@@ -13,7 +13,6 @@
 LAGS = 256
 BLOCK = 32
 CH_DEV = 64
-PIECE = 32
 VMEM_GRANT = 60899328
 
 
@@ -150,12 +149,10 @@
         return np.concatenate([real * scale, imag * scale], axis=1)
 
     whole = table(places, np.ones(half))
-    left, core, right = whole[:reach], whole[reach : reach + span], whole[reach + span :]
     lags = table(shifts, ends).T
     taps = table(shifts, np.ones(half))
     back = table(places[reach : reach + span], ends)
-    halo = np.stack([left, right])
-    return [t.astype(np.float32).astype(jnp.bfloat16) for t in (core, halo, lags, taps, back)]
+    return [t.astype(np.float32).astype(jnp.bfloat16) for t in (whole, lags, taps, back)]
 
 
 def dot(left, right, left_dim=1, right_dim=0):
@@ -176,12 +173,12 @@
 
 
 def fused_kernel(
-    sizes, x_hbm, pairs_hbm, observed_hbm, mask_hbm, core_hbm, halo_hbm, lags_hbm, taps_hbm, back_hbm,
-    out, pairs, core, halo, rest, observed, mask, core_table, halo_table, lags, taps, back,
+    sizes, x_hbm, pairs_hbm, observed_hbm, mask_hbm, whole_hbm, lags_hbm, taps_hbm, back_hbm,
+    out, pairs, ext, observed, mask, whole, lags, taps, back,
     inbox_sum, stage_total, inbox_total, columns, held_spec, core_spec, both_spec, left_spec,
-    full_spec, select, cross, stage_core, inbox_core, stage3, inbox3, inbox4, grads, stage6,
-    following, high, load_sem, send1, recv1, send_sum, recv_sum, total_sem, core_send, core_recv, relay_send, relay_recv,
-    send3, recv3, send4, recv4, send6, recv6,
+    full_spec, select, cross, stage_core, inbox_core, stage3, inbox3, inbox4, grads,
+    following, high, load_sem, send1, recv1, send_sum, recv_sum, total_sem, core_send, core_recv,
+    relay_send, relay_recv, send3, recv3, send4, recv4,
 ):
     fibres, segs, recs = sizes
     bands = fibres * segs
@@ -230,21 +227,6 @@
             bit *= 2
         return result
 
-    class bulk:
-        def __init__(self, first, size, dst, send, recv, device):
-            self.whole = remote(x_hbm.at[rows(first, size, PIECE)], dst, send, recv, device)
-            self.pieces = [
-                remote(x_hbm.at[rows(first + i, PIECE, PIECE)], dst.at[pl.ds(i, PIECE)], send, recv, device)
-                for i in range(0, size, PIECE)
-            ]
-
-        def start(self):
-            for piece in self.pieces:
-                piece.start()
-
-        def wait_send(self):
-            self.whole.wait_send()
-
     partner = at(f, s, 1 - r)
     across = at(f, o, r)
     places = [(fi, si) for fi in range(fibres) for si in range(segs)]
@@ -258,35 +240,60 @@
         def _():
             signal(barrier, at(fi, si, r))
 
-    locals_ = [
-        pltpu.make_async_copy(x_hbm.at[rows(span * s, span, reach)], core.at[s], load_sem.at[0]),
-        pltpu.make_async_copy(x_hbm.at[rows(reach + reach * o, reach, reach)], halo.at[o, s], load_sem.at[1]),
-        pltpu.make_async_copy(x_hbm.at[rows((2 * span - reach) * o, reach, reach)], rest, load_sem.at[2]),
-    ]
     loads = [
-        pltpu.make_async_copy(src, dst, load_sem.at[3 + i])
+        pltpu.make_async_copy(src, dst, load_sem.at[i])
         for i, (src, dst) in enumerate(
             [
-                (pairs_hbm, pairs), (core_hbm, core_table), (halo_hbm, halo_table), (lags_hbm, lags), (observed_hbm.at[r], observed), (mask_hbm, mask), (taps_hbm, taps), (back_hbm, back),
+                (x_hbm, ext.at[s, pl.ds(reach, 2 * span)]), (pairs_hbm, pairs), (whole_hbm, whole), (lags_hbm, lags),
+                (observed_hbm.at[r], observed), (mask_hbm, mask), (taps_hbm, taps), (back_hbm, back),
             ]
         )
     ]
-    for load in locals_ + loads:
+    for load in loads:
         load.start()
+
+    def give(first, size, place, send, recv, device):
+        return remote(
+            x_hbm.at[pl.ds(first, size)], ext.at[s, pl.ds(place, size)], send1.at[send], recv1.at[recv], device
+        )
+
+    needed = [
+        [give(span, span, span + reach, 0, 0, across), give(reach, reach, 2 * reach, 1, 1, across)],
+        [give(0, span, reach, 0, 0, across)],
+    ]
+    later = [give(0, reach, reach, 2, 2, across), give(span, span, reach + span, 2, 2, across)]
+    upper, lower = (f + 1) % fibres, (f + last) % fibres
+    up = give(2 * span - reach, reach, 0, 3, 3, at(upper, s, r))
+    up_across = give(2 * span - reach, reach, 0, 4, 4, at(upper, 0, r))
+    down = give(0, reach, reach + 2 * span, 5, 5, at(lower, s, r))
+    edges = [pl.ds(0, reach), pl.ds(reach + 2 * span, reach)]
+    passed = [
+        remote(ext.at[s, edge], ext.at[s, edge], send1.at[6 + i], recv1.at[6 + i], across)
+        for i, edge in enumerate(edges)
+    ]
+
+    def send_up():
+        up.start()
+
+        @pl.when(s == 1)
+        def _():
+            up_across.start()
+
     pl.semaphore_wait(barrier, segs * (f + 1))
-    after = bulk(
-        2 * span - reach, reach, halo.at[0, s], send1.at[0], recv1.at[2 + s], at((f + 1) % fibres, 0, r)
-    )
-    before = bulk(0, reach, halo.at[1, s], send1.at[1], recv1.at[4 + s], at((f + last) % fibres, 1, r))
-    core_cut = span // 2
-    core_sends = bulk(span * o, span, core.at[s], send1.at[2], recv1.at[0], across)
-    row = bulk(reach + reach * s, reach, halo.at[s, s], send1.at[4], recv1.at[1], across)
-
-    core_sends.start()
-
-    @pl.when(s == 0)
-    def _():
-        row.start()
+    for si in range(segs):
+
+        @pl.when(s == si)
+        def _():
+            for copy in needed[si]:
+                copy.start()
+
+    @pl.when(f > 0)
+    def _():
+        down.start()
+
+    @pl.when(f == last)
+    def _():
+        send_up()
 
     for fi, si in places:
 
@@ -298,11 +305,8 @@
         def _():
             signal(high, at(fi, si, r))
 
-    for load in locals_:
-        load.wait()
-    folded = sum(
-        part.astype(full).reshape(-1, 8, width).sum(axis=0) for part in (core[s], halo[o, s], rest[...])
-    )
+    loads[0].wait()
+    folded = ext[s, pl.ds(reach, 2 * span)].astype(full).reshape(-1, 8, width).sum(axis=0)
     odd = lax.broadcasted_iota(jnp.int32, folded.shape, 0) % 2 == 1
     inbox_sum[band] = jnp.concatenate(
         [
@@ -311,7 +315,7 @@
         ],
         axis=0,
     )
-    sends = [after, before, row, core_sends]
+    sends = [up, down]
     own_sum = inbox_sum.at[band]
     sum_sends = [
         remote(own_sum, own_sum, send_sum.at[fi * segs + si], recv_sum.at[band], at(fi, si, r)) for fi, si in places
@@ -324,7 +328,7 @@
         def _():
             copy.start()
 
-    loads[0].wait()
+    loads[1].wait()
     cut = bands // 2
     near = band // cut
     groups = [(r, near), (r, 1 - near), (1 - r, near), (1 - r, 1 - near)]
@@ -337,26 +341,36 @@
                 first = p * group + (end * cut + i) * BLOCK
                 inside = (lane >= first) & (lane < first + BLOCK)
                 target = jnp.where(inside, lane + (pairs[end, (side * cut + i) * recs + h] * BLOCK - first), target)
-    line = lax.broadcasted_iota(jnp.int32, select.shape, 0)
+    line = lax.broadcasted_iota(jnp.int32, select.shape, 0) + s * width
     select[...] = jnp.where(line == target, 1.0, 0.0).astype(low)
 
     def put(spec, seg, value):
         spec[rows(seg * blocks, blocks, blocks)] = value.astype(low).reshape(blocks, BLOCK, n)
 
     def core_part(seg):
-        part = dot(core[seg], core_table[...], 0, 0)
+        part = dot(ext[seg, rows(reach + span * s, span, reach)], whole[reach : reach + span], 0, 0)
         held_spec[seg] = part
         put(core_spec, seg, part)
 
-    loads[1].wait()
+    def left_part(seg):
+        part = dot(ext[seg, rows(span * s, reach, reach)], whole[:reach], 0, 0)
+        put(left_spec, seg, part)
+        put(both_spec, seg, part + held_spec[seg])
+
+    loads[2].wait()
     core_part(s)
 
     @pl.when(f < last)
     def _():
         pl.semaphore_wait(following, segs)
-
-    after.start()
-    arrived(core.at[o], recv1.at[0])
+        send_up()
+
+    for si in range(segs):
+
+        @pl.when(s == 1 - si)
+        def _():
+            arrived(ext.at[si, pl.ds(reach + span * (1 - si), span)], recv1.at[0])
+
     core_part(o)
 
     @pl.when(f < last - 1)
@@ -371,35 +385,21 @@
 
     @pl.when(f == 0)
     def _():
-        before.start()
-
-    loads[2].wait()
-
-    def left_part(seg):
-        part = dot(halo[0, seg], halo_table[0], 0, 0)
-        put(left_spec, seg, part)
-        part += held_spec[seg]
-        held_spec[seg] = part
-        put(both_spec, seg, part)
+        down.start()
 
     @pl.when(s == 0)
     def _():
-        arrived(halo.at[0, 0], recv1.at[2])
+        arrived(ext.at[0, edges[0]], recv1.at[3])
 
     left_part(s)
 
     @pl.when(s == 0)
     def _():
-        arrived(halo.at[0, 1], recv1.at[3])
+        arrived(ext.at[1, edges[0]], recv1.at[4])
 
     @pl.when(s == 1)
     def _():
-        arrived(halo.at[0, 0], recv1.at[1])
-        row.start()
-
-    @pl.when(f > 0)
-    def _():
-        before.start()
+        arrived(ext.at[0, pl.ds(2 * reach, reach)], recv1.at[1])
 
     left_part(o)
 
@@ -440,6 +440,19 @@
                 spread3[j].start()
 
     inbox3[band] = stage3[band]
+
+    @pl.when(s == 0)
+    def _():
+        later[0].start()
+        passed[0].start()
+
+    @pl.when(s == 1)
+    def _():
+        later[1].start()
+        arrived(ext.at[1, edges[0]], recv1.at[3])
+
+    arrived(ext.at[s, edges[1]], recv1.at[5])
+    passed[1].start()
 
     for d in range(1, bands):
         k = flipped(band, d)
@@ -478,27 +491,30 @@
 
     sends.append(push(own, own, relay_send.at[0], relay_recv.at[band], partner))
 
-    @pl.when(s == 0)
-    def _():
-        arrived(halo.at[1, 1], recv1.at[1])
+    for si in range(segs):
+
+        @pl.when(s == 1 - si)
+        def _():
+            arrived(ext.at[si, pl.ds(reach + span * si, reach + (span - reach) * si)], recv1.at[2])
 
     @pl.when(s == 1)
     def _():
-        for seg in range(segs):
-            arrived(halo.at[1, seg], recv1.at[4 + seg])
-
+        arrived(ext.at[0, edges[0]], recv1.at[6])
+
+    arrived(ext.at[o, edges[1]], recv1.at[7])
     head = lax.broadcasted_iota(jnp.int32, (1, half), 1) == 0
     for seg in range(segs):
         total = jnp.concatenate([stage_total[seg]] * 4, axis=0).T * (n / S)
-        value = held_spec[seg] + dot(halo[1, seg], halo_table[1], 0, 0)
-        value = jnp.concatenate(
-            [
-                value[:, :half] + jnp.where(head, total[:, 0:1], 0.0),
-                value[:, half:] - jnp.where(head, total[:, 1:2], 0.0),
-            ],
-            axis=1,
-        )
-        put(full_spec, seg, value)
+        for w in range(segs):
+            value = dot(ext[seg, pl.ds(span * w, n)], whole[...], 0, 0)
+            value = jnp.concatenate(
+                [
+                    value[:, :half] + jnp.where(head, total[:, 0:1], 0.0),
+                    value[:, half:] - jnp.where(head, total[:, 1:2], 0.0),
+                ],
+                axis=1,
+            )
+            put(full_spec.at[w], seg, value)
     loads[6].wait()
 
     def gradients(p):
@@ -508,15 +524,16 @@
             pair = (side * cut + i) * recs + h
             filters = spread[i * BLOCK : (i + 1) * BLOCK]
             filters = filters[:, :half], filters[:, half:]
-            first = block(full_spec, pairs[0, pair])
-            second = block(full_spec, pairs[1, pair])
             base = p * group + i * BLOCK
-            for start, parts in (
-                (base, spectral_product([(filters, second)], -1.0)),
-                (base + cut * BLOCK, spectral_product([(first, filters)], 1.0)),
-            ):
-                for q in range(2):
-                    grads[pl.ds(start, BLOCK), pl.ds(q * half, half)] = parts[q].astype(low)
+            for w in range(segs):
+                first = block(full_spec.at[w], pairs[0, pair])
+                second = block(full_spec.at[w], pairs[1, pair])
+                for start, parts in (
+                    (base, spectral_product([(filters, second)], -1.0)),
+                    (base + cut * BLOCK, spectral_product([(first, filters)], 1.0)),
+                ):
+                    for q in range(2):
+                        grads[w, pl.ds(start, BLOCK), pl.ds(q * half, half)] = parts[q].astype(low)
 
     for d in range(1, bands):
         k = flipped(band, d)
@@ -530,14 +547,20 @@
         gradients(p)
     loads[7].wait()
 
-    def summed(seg):
-        return dot(select[rows(seg * width, width, width), :], grads[...]).astype(low)
-
-    stage6[...] = dot(back[...], summed(o), 1, 1).astype(low)
-    here = rows(span * s, span, span)
-    sends.append(push(stage6, out.at[here, :], send6.at[0], recv6.at[0], across))
-    out[here, :] = dot(back[...], summed(s), 1, 1).astype(low)
-    arrived(out.at[rows(span * o, span, span), :], recv6.at[0])
+    for w in range(segs):
+        summed = dot(select[...], grads[w]).astype(low)
+        out[pl.ds(span * w, span), :] = dot(back[...], summed, 1, 1).astype(low)
+    for si in range(segs):
+
+        @pl.when(s == si)
+        def _():
+            for copy in needed[si] + [later[si]] + passed[si:]:
+                copy.wait_send()
+
+    @pl.when(s == 1)
+    def _():
+        up_across.wait_send()
+
     for copy in sends:
         copy.wait_send()
     for j in range(bands):
@@ -567,7 +590,7 @@
     vmem = pl.BlockSpec(memory_space=pltpu.VMEM)
     hbm = pl.BlockSpec(memory_space=pltpu.HBM)
     corr = (BLOCK, LAGS)
-    spec = pltpu.VMEM((total // BLOCK, BLOCK, n), low)
+    spec = (total // BLOCK, BLOCK, n)
 
     def sems(*sizes):
         return [pltpu.SemaphoreType.DMA((size,)) for size in sizes]
@@ -575,17 +598,14 @@
     result = pl.pallas_call(
         functools.partial(fused_kernel, (fibres, segs, recs)),
         out_shape=pltpu.VMEM((extent, width), low),
-        in_specs=[hbm] * 9,
+        in_specs=[hbm] * 8,
         out_specs=vmem,
         scratch_shapes=[
             pltpu.SMEM((2, pairs.shape[0]), jnp.int32),
-            pltpu.VMEM((segs, span, width), low),
-            pltpu.VMEM((2, segs, reach, width), low),
-            pltpu.VMEM((reach, width), low),
+            pltpu.VMEM((segs, 2 * span + 2 * reach, width), low),
             pltpu.VMEM(corr, full),
             pltpu.VMEM(lag_mask.shape, jnp.int32),
-            pltpu.VMEM((span, n), low),
-            pltpu.VMEM((2, reach, n), low),
+            pltpu.VMEM((n, n), low),
             pltpu.VMEM((n, LAGS), low),
             pltpu.VMEM((LAGS, n), low),
             pltpu.VMEM((span, n), low),
@@ -594,20 +614,21 @@
             pltpu.VMEM((segs, 2, width), full),
             pltpu.VMEM((total // BLOCK, BLOCK, 8), full),
             pltpu.VMEM((segs, width, n), full),
-            spec, spec, spec, spec,
-            pltpu.VMEM((total, 2 * count), low),
+            pltpu.VMEM(spec, low),
+            pltpu.VMEM(spec, low),
+            pltpu.VMEM(spec, low),
+            pltpu.VMEM((segs,) + spec, low),
+            pltpu.VMEM((width, 2 * count), low),
             pltpu.VMEM((2 * recs, own // 2, n), low),
             pltpu.VMEM((2, own // 2, LAGS), low),
             pltpu.VMEM((2, own // 2, LAGS), low),
             pltpu.VMEM((bands,) + corr, low),
             pltpu.VMEM((bands,) + corr, low),
             pltpu.VMEM((recs, bands) + corr, low),
-            pltpu.VMEM((2 * count, n), low),
-            pltpu.VMEM((span, width), low),
+            pltpu.VMEM((segs, 2 * count, n), low),
             pltpu.SemaphoreType.REGULAR,
             pltpu.SemaphoreType.REGULAR,
-            *sems(11, 5, 8, bands + 1, bands, 2, 2, 2, bands, bands),
-            *sems(bands, bands, bands, bands, 2, 2),
+            *sems(8, 8, 8, bands + 1, bands, 2, 2, 2, bands, bands, bands, bands, bands, bands),
         ],
         compiler_params=pltpu.CompilerParams(
             has_side_effects=True, collective_id=0, vmem_limit_bytes=VMEM_GRANT

time: 30.4 us -> 26.5 us (0.87)
  Pallas kernels: 29.5 us -> 25.6 us
    pallas_call x1, Pallas kernels: 29.5 us -> 25.6 us  [fused_on_device(): pl.pallas_call(functools.partial(fused_kernel, (fibres, segs, recs)), out...]
where the time goes in v5:
time: 26.5 us; the launch traced here: 26.3 us
  Pallas kernels  25.6 us (97%)
  local copies, waits for them, and re-layouts  0.71 us (3%)
    pallas_call x1, Pallas kernels, fused_on_device(): pl.pallas_call(functools.partial(fused_kernel, (fibres, segs, recs)), out...  25.6 us
    unnamed x1, local copies, waits for them, and re-layouts  0.71 us

profile of v5, /device:TPU:0, one launch (start us, length us, event | category | flops | bytes accessed | tf_op | source)
XLA Modules:
  0.0 26.3 jit_solution(5332514655529120478)
XLA Ops:
  0.0 25.6 %adjoint.1 = bf16[512,256]{1,0:T(8,128)(2,1)S(1)} custom-call(bf16[512,256]{1,0:T(8,128)(2,1)} %bitcast.4, s32[2,16]{1,0:T(2,128)} %bitcast.5, f32[2,32,256]{2,1,0:T(8,128)} %observed_hbm.1, s32[2,256]{1,0:T(2,128)} %mask_hbm.1, bf16[512,512]{1,0:T(8,128)(2,1)} %constant.8.clone.whole_hbm, bf16[512,256]{1,0:T(8,128)(2,1)} %constant.9.clone.lags_hbm, ...), custom_call_target="tpu_custom_call" | custom-call | tf_op jit(solution)/shard_map/adjoint/pallas_call | solution.py:598
  25.6 0.7 %copy.10 = bf16[1,512,256]{2,1,0:T(8,128)(2,1)} copy(bf16[1,512,256]{2,1,0:T(8,128)(2,1)S(1)} %bitcast.3) | data formatting | bytes 524288

commit v6 on v5

--- a/solution.py
+++ b/solution.py
@@ -168,8 +168,12 @@
     both = sum(p1 * q1 for (_, p1), (_, q1) in terms)
     real = sum(p0 * q0 for (p0, _), (q0, _) in terms)
     imag = sum(p1 * q0 - sign * (p0 * q1) for (p0, p1), (q0, q1) in terms)
-    ends = lax.broadcasted_iota(jnp.int32, both.shape, 1) == 0
-    return real + jnp.where(ends, 0.0, sign * both), jnp.where(ends, both, imag)
+    whole = real + sign * both
+    ends = lax.broadcasted_iota(jnp.int32, (both.shape[0], 128), 1) == 0
+    return tuple(
+        jnp.concatenate([jnp.where(ends, end[:, :128], value[:, :128]), value[:, 128:]], axis=1)
+        for end, value in ((real, whole), (both, imag))
+    )
 
 
 def fused_kernel(
@@ -273,7 +277,9 @@
     ]
 
     def send_up():
-        up.start()
+        @pl.when(s == 0)
+        def _():
+            up.start()
 
         @pl.when(s == 1)
         def _():
@@ -286,10 +292,6 @@
         def _():
             for copy in needed[si]:
                 copy.start()
-
-    @pl.when(f > 0)
-    def _():
-        down.start()
 
     @pl.when(f == last)
     def _():
@@ -383,9 +385,20 @@
         def _():
             copy.start()
 
-    @pl.when(f == 0)
-    def _():
-        down.start()
+    @pl.when(s == 1)
+    def _():
+        up.start()
+
+    down.start()
+
+    def send_later():
+        for si in range(segs):
+
+            @pl.when(s == si)
+            def _():
+                later[si].start()
+
+    pl.when(f == 0)(send_later)
 
     @pl.when(s == 0)
     def _():
@@ -401,15 +414,19 @@
     def _():
         arrived(ext.at[0, pl.ds(2 * reach, reach)], recv1.at[1])
 
+    pl.when(f > 0)(send_later)
     left_part(o)
 
     def block(spec, index):
         value = spec[index].astype(full)
         return value[:, :half], value[:, half:]
 
-    def correlate(place, h, side):
-        for i in range(cut):
-            pair = (side * cut + i) * recs + h
+    ordered = sorted(range(bands), key=lambda j: (-abs(2 * (j // segs) - last), -j))
+    chunks = ordered[:cut], ordered[cut:]
+
+    def correlate(place, h, chunk):
+        for i, j in enumerate(chunk):
+            pair = j * recs + h
             one, two = pairs[0, pair], pairs[1, pair]
             terms = [(block(core_spec, one), block(both_spec, two)), (block(left_spec, one), block(core_spec, two))]
             real, imag = spectral_product(terms, 1.0)
@@ -419,21 +436,20 @@
         return dot(cross[place], lags[...])
 
     loads[3].wait()
-    sides = (1, 0)
-    for i, side in enumerate(sides):
-        stage_core[i] = correlate(i, 1 - r, side).astype(low)
+    for i, chunk in enumerate(chunks):
+        stage_core[i] = correlate(i, 1 - r, chunk).astype(low)
         sends.append(push(stage_core.at[i], inbox_core.at[i], core_send.at[i], core_recv.at[i], partner))
 
     spread3 = [
         remote(stage3.at[j], inbox3.at[band], send3.at[j], recv3.at[band], at(j // segs, j % segs, r))
         for j in range(bands)
     ]
-    for i, side in enumerate(sides):
-        partial = correlate(2 + i, r, side)
+    for i, chunk in enumerate(chunks):
+        partial = correlate(2 + i, r, chunk)
         arrived(inbox_core.at[i], core_recv.at[i])
         partial = (partial + inbox_core[i].astype(full)).astype(low)
-        stage3[rows(side * cut, cut, cut)] = partial.reshape(cut, BLOCK, LAGS)
-        for j in range((side + 1) * cut - 1, side * cut - 1, -1):
+        for place, j in enumerate(chunk):
+            stage3[j] = partial[place * BLOCK : (place + 1) * BLOCK]
 
             @pl.when(band != j)
             def _():
@@ -443,12 +459,10 @@
 
     @pl.when(s == 0)
     def _():
-        later[0].start()
         passed[0].start()
 
     @pl.when(s == 1)
     def _():
-        later[1].start()
         arrived(ext.at[1, edges[0]], recv1.at[3])
 
     arrived(ext.at[s, edges[1]], recv1.at[5])

time: 26.5 us -> 25.3 us (0.955)
  Pallas kernels: 25.6 us -> 24.4 us
    pallas_call x1, Pallas kernels: 25.6 us -> 24.4 us  [fused_on_device(): pl.pallas_call(functools.partial(fused_kernel, (fibres, segs, recs)), out...]
where the time goes in v6:
time: 25.3 us; the launch traced here: 25.2 us
  Pallas kernels  24.4 us (96%)
  local copies, waits for them, and re-layouts  0.71 us (3%)
    pallas_call x1, Pallas kernels, fused_on_device(): pl.pallas_call(functools.partial(fused_kernel, (fibres, segs, recs)), out...  24.4 us
    unnamed x1, local copies, waits for them, and re-layouts  0.71 us

profile of v6, /device:TPU:0, one launch (start us, length us, event | category | flops | bytes accessed | tf_op | source)
XLA Modules:
  0.0 25.2 jit_solution(16106556253571991554)
XLA Ops:
  0.0 24.4 %adjoint.1 = bf16[512,256]{1,0:T(8,128)(2,1)S(1)} custom-call(bf16[512,256]{1,0:T(8,128)(2,1)} %bitcast.4, s32[2,16]{1,0:T(2,128)} %bitcast.5, f32[2,32,256]{2,1,0:T(8,128)} %observed_hbm.1, s32[2,256]{1,0:T(2,128)} %mask_hbm.1, bf16[512,512]{1,0:T(8,128)(2,1)} %constant.8.clone.whole_hbm, bf16[512,256]{1,0:T(8,128)(2,1)} %constant.9.clone.lags_hbm, ...), custom_call_target="tpu_custom_call" | custom-call | tf_op jit(solution)/shard_map/adjoint/pallas_call | solution.py:612
  24.5 0.7 %copy.10 = bf16[1,512,256]{2,1,0:T(8,128)(2,1)} copy(bf16[1,512,256]{2,1,0:T(8,128)(2,1)S(1)} %bitcast.3) | data formatting | bytes 524288

commit v7 on v6

--- a/solution.py
+++ b/solution.py
@@ -152,6 +152,7 @@
     lags = table(shifts, ends).T
     taps = table(shifts, np.ones(half))
     back = table(places[reach : reach + span], ends)
+    lags = np.concatenate([lags, lags])
     return [t.astype(np.float32).astype(jnp.bfloat16) for t in (whole, lags, taps, back)]
 
 
@@ -164,22 +165,22 @@
     )
 
 
-def spectral_product(terms, sign):
+def spectral_product(terms, sign, extra=None):
     both = sum(p1 * q1 for (_, p1), (_, q1) in terms)
     real = sum(p0 * q0 for (p0, _), (q0, _) in terms)
     imag = sum(p1 * q0 - sign * (p0 * q1) for (p0, p1), (q0, q1) in terms)
     whole = real + sign * both
     ends = lax.broadcasted_iota(jnp.int32, (both.shape[0], 128), 1) == 0
     return tuple(
-        jnp.concatenate([jnp.where(ends, end[:, :128], value[:, :128]), value[:, 128:]], axis=1)
-        for end, value in ((real, whole), (both, imag))
+        jnp.concatenate([jnp.where(ends, end, value[:, :128]), value[:, 128:]], axis=1)
+        for end, value in ((real[:, :128], whole), (both[:, :128] if extra is None else both[:, :128] + extra, imag))
     )
 
 
 def fused_kernel(
     sizes, x_hbm, pairs_hbm, observed_hbm, mask_hbm, whole_hbm, lags_hbm, taps_hbm, back_hbm,
     out, pairs, ext, observed, mask, whole, lags, taps, back,
-    inbox_sum, stage_total, inbox_total, columns, held_spec, core_spec, both_spec, left_spec,
+    inbox_sum, stage_total, inbox_total, columns, core_spec, both_spec, left_spec,
     full_spec, select, cross, stage_core, inbox_core, stage3, inbox3, inbox4, grads,
     following, high, load_sem, send1, recv1, send_sum, recv_sum, total_sem, core_send, core_recv,
     relay_send, relay_recv, send3, recv3, send4, recv4,
@@ -308,15 +309,13 @@
             signal(high, at(fi, si, r))
 
     loads[0].wait()
-    folded = ext[s, pl.ds(reach, 2 * span)].astype(full).reshape(-1, 8, width).sum(axis=0)
-    odd = lax.broadcasted_iota(jnp.int32, folded.shape, 0) % 2 == 1
-    inbox_sum[band] = jnp.concatenate(
-        [
-            jnp.sum(folded, axis=0, keepdims=True),
-            jnp.sum(jnp.where(odd, -folded, folded), axis=0, keepdims=True),
-        ],
-        axis=0,
-    )
+    folded = [
+        ext[s, pl.ds(reach + span * w, span)].astype(full).reshape(-1, 8, width).sum(axis=0) for w in range(segs)
+    ]
+    odd = lax.broadcasted_iota(jnp.int32, (8, width), 0) % 2 == 1
+    flat = jnp.sum(folded[0] + folded[1], axis=0, keepdims=True)
+    turned = [jnp.sum(jnp.where(odd, -part, part), axis=0, keepdims=True) for part in folded]
+    inbox_sum[band] = jnp.concatenate([flat] + turned + [jnp.zeros_like(flat)], axis=0)
     sends = [up, down]
     own_sum = inbox_sum.at[band]
     sum_sends = [
@@ -347,17 +346,16 @@
     select[...] = jnp.where(line == target, 1.0, 0.0).astype(low)
 
     def put(spec, seg, value):
-        spec[rows(seg * blocks, blocks, blocks)] = value.astype(low).reshape(blocks, BLOCK, n)
+        spec[rows(seg * blocks, blocks, blocks)] = value.astype(spec.dtype).reshape(blocks, BLOCK, n)
 
     def core_part(seg):
         part = dot(ext[seg, rows(reach + span * s, span, reach)], whole[reach : reach + span], 0, 0)
-        held_spec[seg] = part
         put(core_spec, seg, part)
 
     def left_part(seg):
         part = dot(ext[seg, rows(span * s, reach, reach)], whole[:reach], 0, 0)
         put(left_spec, seg, part)
-        put(both_spec, seg, part + held_spec[seg])
+        put(both_spec, seg, part + core_spec[rows(seg * blocks, blocks, blocks)].reshape(width, n))
 
     loads[2].wait()
     core_part(s)
@@ -429,10 +427,13 @@
             pair = j * recs + h
             one, two = pairs[0, pair], pairs[1, pair]
             terms = [(block(core_spec, one), block(both_spec, two)), (block(left_spec, one), block(core_spec, two))]
-            real, imag = spectral_product(terms, 1.0)
-            here = pl.ds(i * BLOCK, BLOCK)
-            cross[place, here, pl.ds(0, half)] = real.astype(low)
-            cross[place, here, pl.ds(half, half)] = imag.astype(low)
+            inner = terms[0][0][1][:, :128] * terms[1][1][1][:, :128]
+            parts = spectral_product(terms, 1.0, inner * (-n / span))
+            for q, part in enumerate(parts):
+                high_part = part.astype(low)
+                here = pl.ds(i * BLOCK, BLOCK)
+                cross[place, here, pl.ds(q * half, half)] = high_part
+                cross[place, here, pl.ds(n + q * half, half)] = (part - high_part.astype(full)).astype(low)
         return dot(cross[place], lags[...])
 
     loads[3].wait()
@@ -472,19 +473,31 @@
         k = flipped(band, d)
         arrived(inbox_sum.at[k], recv_sum.at[k])
     for seg in range(segs):
-        stage_total[seg] = sum(inbox_sum[fi * segs + seg] for fi in range(fibres))
+        told = [inbox_sum[fi * segs + seg] for fi in range(fibres)]
+        spans = jnp.concatenate([part[1:3] for part in told], axis=0)
+        stage_total[seg] = jnp.concatenate(
+            [
+                sum(part[0:1] for part in told),
+                jnp.sum(spans, axis=0, keepdims=True),
+                spans,
+                jnp.zeros((2 * bands - 2 - 2 * fibres, width), full),
+            ],
+            axis=0,
+        )
     sends.append(push(stage_total, inbox_total, total_sem.at[0], total_sem.at[1], partner))
     arrived(inbox_total, total_sem.at[1])
     for seg in range(segs):
-        total = jnp.concatenate([stage_total[seg], inbox_total[seg]] * 2, axis=0)
-        columns[pl.ds(seg * blocks, blocks)] = total.T.reshape(blocks, BLOCK, 8)
+        total = jnp.concatenate([stage_total[seg], inbox_total[seg]], axis=0)
+        columns[pl.ds(seg * blocks, blocks)] = total.T.reshape(blocks, BLOCK, 4 * bands)
     loads[4].wait()
     loads[5].wait()
-    ends = columns[pairs[0, band * recs + r]] * columns[pairs[1, band * recs + r]]
-    flat = ends[:, 0:1] + ends[:, 2:3]
-    alternating = ends[:, 1:2] + ends[:, 3:4]
+    ends = columns[pairs[0, band * recs + r]] * columns[pairs[1, band * recs + r]] * (1.0 / (2.0 * F**0.5))
+    kind = lax.broadcasted_iota(jnp.int32, ends.shape, 1) % (2 * bands)
+    flat = jnp.sum(jnp.where(kind == 0, ends * (1.0 / S), 0.0), axis=1, keepdims=True)
+    turned = jnp.where(kind == 1, ends * (-1.0 / S), ends * (1.0 / span))
+    turned = jnp.sum(jnp.where(kind == 0, 0.0, turned), axis=1, keepdims=True)
     even = lax.broadcasted_iota(jnp.int32, (BLOCK, LAGS), 1) % 2 == reach % 2
-    offset = (flat + jnp.where(even, -alternating, alternating)) * (1.0 / (2.0 * S * F**0.5))
+    offset = flat + jnp.where(even, turned, -turned)
     for d in range(1, bands):
         k = flipped(band, d)
         arrived(inbox3.at[k], recv3.at[k])
@@ -518,7 +531,7 @@
     arrived(ext.at[o, edges[1]], recv1.at[7])
     head = lax.broadcasted_iota(jnp.int32, (1, half), 1) == 0
     for seg in range(segs):
-        total = jnp.concatenate([stage_total[seg]] * 4, axis=0).T * (n / S)
+        total = stage_total[seg].T * (n / S)
         for w in range(segs):
             value = dot(ext[seg, pl.ds(span * w, n)], whole[...], 0, 0)
             value = jnp.concatenate(
@@ -620,20 +633,19 @@
             pltpu.VMEM(corr, full),
             pltpu.VMEM(lag_mask.shape, jnp.int32),
             pltpu.VMEM((n, n), low),
-            pltpu.VMEM((n, LAGS), low),
+            pltpu.VMEM((2 * n, LAGS), low),
             pltpu.VMEM((LAGS, n), low),
             pltpu.VMEM((span, n), low),
-            pltpu.VMEM((bands, 2, width), full),
-            pltpu.VMEM((segs, 2, width), full),
-            pltpu.VMEM((segs, 2, width), full),
-            pltpu.VMEM((total // BLOCK, BLOCK, 8), full),
-            pltpu.VMEM((segs, width, n), full),
-            pltpu.VMEM(spec, low),
-            pltpu.VMEM(spec, low),
-            pltpu.VMEM(spec, low),
+            pltpu.VMEM((bands, 4, width), full),
+            pltpu.VMEM((segs, 2 * bands, width), full),
+            pltpu.VMEM((segs, 2 * bands, width), full),
+            pltpu.VMEM((total // BLOCK, BLOCK, 4 * bands), full),
+            pltpu.VMEM(spec, full),
+            pltpu.VMEM(spec, full),
+            pltpu.VMEM(spec, full),
             pltpu.VMEM((segs,) + spec, low),
             pltpu.VMEM((width, 2 * count), low),
-            pltpu.VMEM((2 * recs, own // 2, n), low),
+            pltpu.VMEM((2 * recs, own // 2, 2 * n), low),
             pltpu.VMEM((2, own // 2, LAGS), low),
             pltpu.VMEM((2, own // 2, LAGS), low),
             pltpu.VMEM((bands,) + corr, low),

time: 25.3 us -> 25.5 us (level)
  Pallas kernels: 24.4 us -> 24.7 us
where the time goes in v7:
time: 25.5 us; the launch traced here: 25.4 us
  Pallas kernels  24.7 us (97%)
  local copies, waits for them, and re-layouts  0.71 us (3%)
    pallas_call x1, Pallas kernels, fused_on_device(): pl.pallas_call(functools.partial(fused_kernel, (fibres, segs, recs)), out...  24.7 us
    unnamed x1, local copies, waits for them, and re-layouts  0.71 us

profile of v7, /device:TPU:0, one launch (start us, length us, event | category | flops | bytes accessed | tf_op | source)
XLA Modules:
  0.0 25.4 jit_solution(7193571415366835167)
XLA Ops:
  0.0 24.7 %adjoint.1 = bf16[512,256]{1,0:T(8,128)(2,1)S(1)} custom-call(bf16[512,256]{1,0:T(8,128)(2,1)} %bitcast.4, s32[2,16]{1,0:T(2,128)} %bitcast.5, f32[2,32,256]{2,1,0:T(8,128)} %observed_hbm.1, s32[2,256]{1,0:T(2,128)} %mask_hbm.1, bf16[512,512]{1,0:T(8,128)(2,1)} %constant.8.clone.whole_hbm, bf16[1024,256]{1,0:T(8,128)(2,1)} %constant.9.clone.lags_hbm, ...), custom_call_target="tpu_custom_call" | custom-call | tf_op jit(solution)/shard_map/adjoint/pallas_call | solution.py:625
  24.7 0.7 %copy.10 = bf16[1,512,256]{2,1,0:T(8,128)(2,1)} copy(bf16[1,512,256]{2,1,0:T(8,128)(2,1)S(1)} %bitcast.3) | data formatting | bytes 524288

commit v8 on v7

--- a/solution.py
+++ b/solution.py
@@ -181,7 +181,7 @@
     sizes, x_hbm, pairs_hbm, observed_hbm, mask_hbm, whole_hbm, lags_hbm, taps_hbm, back_hbm,
     out, pairs, ext, observed, mask, whole, lags, taps, back,
     inbox_sum, stage_total, inbox_total, columns, core_spec, both_spec, left_spec,
-    full_spec, select, cross, stage_core, inbox_core, stage3, inbox3, inbox4, grads,
+    full_spec, select, cross, stage_core, inbox_core, stage3, inbox3, inbox4, grads, held,
     following, high, load_sem, send1, recv1, send_sum, recv_sum, total_sem, core_send, core_recv,
     relay_send, relay_recv, send3, recv3, send4, recv4,
 ):
@@ -331,17 +331,17 @@
 
     loads[1].wait()
     cut = bands // 2
-    near = band // cut
-    groups = [(r, near), (r, 1 - near), (1 - r, near), (1 - r, 1 - near)]
-    group = 2 * cut * BLOCK
+    others = [flipped(band, k * segs) // segs for k in range(1, fibres)]
+    entries = [(r, f), (1 - r, f)] + [(r, fibre) for fibre in others] + [(1 - r, fibre) for fibre in others]
+    group = 2 * segs * BLOCK
     lane = lax.broadcasted_iota(jnp.int32, (1, 2 * count), 1)
     target = lane
-    for p, (h, side) in enumerate(groups):
+    for p, (h, fibre) in enumerate(entries):
         for end in range(2):
-            for i in range(cut):
-                first = p * group + (end * cut + i) * BLOCK
+            for i in range(segs):
+                first = p * group + (end * segs + i) * BLOCK
                 inside = (lane >= first) & (lane < first + BLOCK)
-                target = jnp.where(inside, lane + (pairs[end, (side * cut + i) * recs + h] * BLOCK - first), target)
+                target = jnp.where(inside, lane + (pairs[end, (fibre * segs + i) * recs + h] * BLOCK - first), target)
     line = lax.broadcasted_iota(jnp.int32, select.shape, 0) + s * width
     select[...] = jnp.where(line == target, 1.0, 0.0).astype(low)
 
@@ -544,39 +544,87 @@
             put(full_spec.at[w], seg, value)
     loads[6].wait()
 
-    def gradients(p):
-        h, side = groups[p]
-        spread = dot(inbox4[h, pl.ds(side * cut, cut)].reshape(cut * BLOCK, LAGS), taps[...])
-        for i in range(cut):
-            pair = (side * cut + i) * recs + h
-            filters = spread[i * BLOCK : (i + 1) * BLOCK]
-            filters = filters[:, :half], filters[:, half:]
-            base = p * group + i * BLOCK
-            for w in range(segs):
-                first = block(full_spec.at[w], pairs[0, pair])
-                second = block(full_spec.at[w], pairs[1, pair])
-                for start, parts in (
-                    (base, spectral_product([(filters, second)], -1.0)),
-                    (base + cut * BLOCK, spectral_product([(first, filters)], 1.0)),
-                ):
-                    for q in range(2):
-                        grads[w, pl.ds(start, BLOCK), pl.ds(q * half, half)] = parts[q].astype(low)
-
-    for d in range(1, bands):
-        k = flipped(band, d)
-        arrived(inbox4.at[r, k], recv4.at[k])
-        got = inbox4.at[r, k]
-        sends.append(push(got, got, relay_send.at[d], relay_recv.at[k], partner))
-    for p, (first, stop) in enumerate(((0, 0), (0, 0), (0, cut), (cut, bands))):
-        for d in range(first, stop):
-            k = flipped(band, d)
-            arrived(inbox4.at[1 - r, k], relay_recv.at[k])
-        gradients(p)
+    def gradients(first, stop):
+        given = [inbox4[h, pl.ds(fibre * segs, segs)].reshape(segs * BLOCK, LAGS) for h, fibre in entries[first:stop]]
+        spread = dot(jnp.concatenate(given, axis=0), taps[...])
+        for p in range(first, stop):
+            h, fibre = entries[p]
+            for i in range(segs):
+                pair = (fibre * segs + i) * recs + h
+                start = ((p - first) * segs + i) * BLOCK
+                filters = spread[start : start + BLOCK]
+                filters = filters[:, :half], filters[:, half:]
+                base = p * group + i * BLOCK
+                for w in range(segs):
+                    one = block(full_spec.at[w], pairs[0, pair])
+                    two = block(full_spec.at[w], pairs[1, pair])
+                    for place, parts in (
+                        (base, spectral_product([(filters, two)], -1.0)),
+                        (base + segs * BLOCK, spectral_product([(one, filters)], 1.0)),
+                    ):
+                        for q in range(2):
+                            grads[w, pl.ds(place, BLOCK), pl.ds(q * half, half)] = parts[q].astype(low)
+
+    turns = [flipped(band, d) for d in range(bands)]
+    relays = [
+        remote(inbox4.at[r, k], inbox4.at[r, k], relay_send.at[d], relay_recv.at[k], partner)
+        for d, k in enumerate(turns)
+    ]
+    sends += relays[1:]
+
+    def take(d):
+        arrived(inbox4.at[r, turns[d]], recv4.at[turns[d]])
+        relays[d].start()
+
+    def relayed(d):
+        arrived(inbox4.at[1 - r, turns[d]], relay_recv.at[turns[d]])
+
+    def fibre_first():
+        for d in range(segs):
+            relayed(d)
+        gradients(0, recs)
+
+    def gather(first, stop):
+        cut_at = slice(first * group, stop * group)
+        return [dot(select[:, cut_at], grads[w, cut_at]) for w in range(segs)]
+
+    direct = recs + fibres - 1
+    for d in range(1, segs):
+        take(d)
+
+    @pl.when(r == 0)
+    def _():
+        fibre_first()
+        for w, part in enumerate(gather(0, recs)):
+            held[w] = part
+
+    for d in range(segs, bands):
+        take(d)
+
+    @pl.when(r == 1)
+    def _():
+        fibre_first()
+        gradients(recs, direct)
+        for w, part in enumerate(gather(0, direct)):
+            held[w] = part
+
+    @pl.when(r == 0)
+    def _():
+        gradients(recs, direct)
+
+    for d in range(segs, bands):
+        relayed(d)
+    gradients(direct, recs * fibres)
     loads[7].wait()
 
-    for w in range(segs):
-        summed = dot(select[...], grads[w]).astype(low)
-        out[pl.ds(span * w, span), :] = dot(back[...], summed, 1, 1).astype(low)
+    for core, first in enumerate((recs, direct)):
+
+        @pl.when(r == core)
+        def _():
+            for w, part in enumerate(gather(first, recs * fibres)):
+                summed = (held[w] + part).astype(low)
+                out[pl.ds(span * w, span), :] = dot(back[...], summed, 1, 1).astype(low)
+
     for si in range(segs):
 
         @pl.when(s == si)
@@ -652,6 +700,7 @@
             pltpu.VMEM((bands,) + corr, low),
             pltpu.VMEM((recs, bands) + corr, low),
             pltpu.VMEM((segs, 2 * count, n), low),
+            pltpu.VMEM((segs, width, n), full),
             pltpu.SemaphoreType.REGULAR,
             pltpu.SemaphoreType.REGULAR,
             *sems(8, 8, 8, bands + 1, bands, 2, 2, 2, bands, bands, bands, bands, bands, bands),

time: 25.5 us -> 25.1 us (0.984)
  Pallas kernels: 24.7 us -> 24.1 us
    pallas_call x1, Pallas kernels: 24.7 us -> 24.1 us  [fused_on_device(): pl.pallas_call(functools.partial(fused_kernel, (fibres, segs, recs)), out...]
where the time goes in v8:
time: 25.1 us; the launch traced here: 24.8 us
  Pallas kernels  24.1 us (96%)
  local copies, waits for them, and re-layouts  0.71 us (3%)
    pallas_call x1, Pallas kernels, fused_on_device(): pl.pallas_call(functools.partial(fused_kernel, (fibres, segs, recs)), out...  24.1 us
    unnamed x1, local copies, waits for them, and re-layouts  0.71 us

profile of v8, /device:TPU:0, one launch (start us, length us, event | category | flops | bytes accessed | tf_op | source)
XLA Modules:
  0.0 24.8 jit_solution(15978619133786286551)
XLA Ops:
  0.0 24.1 %adjoint.1 = bf16[512,256]{1,0:T(8,128)(2,1)S(1)} custom-call(bf16[512,256]{1,0:T(8,128)(2,1)} %bitcast.4, s32[2,16]{1,0:T(2,128)} %bitcast.5, f32[2,32,256]{2,1,0:T(8,128)} %observed_hbm.1, s32[2,256]{1,0:T(2,128)} %mask_hbm.1, bf16[512,512]{1,0:T(8,128)(2,1)} %constant.8.clone.whole_hbm, bf16[1024,256]{1,0:T(8,128)(2,1)} %constant.9.clone.lags_hbm, ...), custom_call_target="tpu_custom_call" | custom-call | tf_op jit(solution)/shard_map/adjoint/pallas_call | solution.py:673
  24.1 0.7 %copy.10 = bf16[1,512,256]{2,1,0:T(8,128)(2,1)} copy(bf16[1,512,256]{2,1,0:T(8,128)(2,1)S(1)} %bitcast.3) | data formatting | bytes 524288

commit v9 on v8

--- a/solution.py
+++ b/solution.py
@@ -510,13 +510,13 @@
     spread4 = [
         remote(own, own, send4.at[j], recv4.at[band], at(j // segs, j % segs, r)) for j in range(bands)
     ]
+    sends.append(push(own, own, relay_send.at[0], relay_recv.at[band], partner))
     for j in range(bands):
 
         @pl.when(band != j)
         def _():
             spread4[j].start()
 
-    sends.append(push(own, own, relay_send.at[0], relay_recv.at[band], partner))
 
     for si in range(segs):
 
@@ -608,19 +608,14 @@
         for w, part in enumerate(gather(0, direct)):
             held[w] = part
 
-    @pl.when(r == 0)
-    def _():
-        gradients(recs, direct)
-
+    loads[7].wait()
     for d in range(segs, bands):
         relayed(d)
-    gradients(direct, recs * fibres)
-    loads[7].wait()
-
     for core, first in enumerate((recs, direct)):
 
         @pl.when(r == core)
         def _():
+            gradients(first, recs * fibres)
             for w, part in enumerate(gather(first, recs * fibres)):
                 summed = (held[w] + part).astype(low)
                 out[pl.ds(span * w, span), :] = dot(back[...], summed, 1, 1).astype(low)

time: 25.1 us -> 25.1 us (level)
  no operation moved by 1% of the time
where the time goes in v9:
time: 25.1 us; the launch traced here: 24.7 us
  Pallas kernels  24 us (96%)
  local copies, waits for them, and re-layouts  0.71 us (3%)
    pallas_call x1, Pallas kernels, fused_on_device(): pl.pallas_call(functools.partial(fused_kernel, (fibres, segs, recs)), out...  24 us
    unnamed x1, local copies, waits for them, and re-layouts  0.71 us

profile of v9, /device:TPU:0, one launch (start us, length us, event | category | flops | bytes accessed | tf_op | source)
XLA Modules:
  0.0 24.7 jit_solution(7207820790222401235)
XLA Ops:
  0.0 24.0 %adjoint.1 = bf16[512,256]{1,0:T(8,128)(2,1)S(1)} custom-call(bf16[512,256]{1,0:T(8,128)(2,1)} %bitcast.4, s32[2,16]{1,0:T(2,128)} %bitcast.5, f32[2,32,256]{2,1,0:T(8,128)} %observed_hbm.1, s32[2,256]{1,0:T(2,128)} %mask_hbm.1, bf16[512,512]{1,0:T(8,128)(2,1)} %constant.8.clone.whole_hbm, bf16[1024,256]{1,0:T(8,128)(2,1)} %constant.9.clone.lags_hbm, ...), custom_call_target="tpu_custom_call" | custom-call | tf_op jit(solution)/shard_map/adjoint/pallas_call | solution.py:668
  24.0 0.7 %copy.10 = bf16[1,512,256]{2,1,0:T(8,128)(2,1)} copy(bf16[1,512,256]{2,1,0:T(8,128)(2,1)S(1)} %bitcast.3) | data formatting | bytes 524288
